TPU v7x, 32 devices: a whole 2x2x4 slice. The times are simulated.
32 devices in a mesh: chord: 4 (over z), span: 8 (over y, x, core).
Axes of the slice: x: 2, y: 2, z: 4, core: 2. Of those that a mesh axis runs over, the one named last changes fastest.
Arguments:
- state: float32 [5, 125, 16, 16, 128], P(None, None, 'chord', 'span'), may hold values from -10 to 10
Outputs:
- residual: float32 [5, 125, 16, 16, 128], P(None, None, 'chord', 'span')
- viscosity: float32 [125, 16, 16, 128], P(None, 'chord', 'span')
All inputs are finite; a program needn't handle non-finite values.
Results may differ from a plain program's by a relative error of at most 0.0001.
Values sent between devices are 32-bit elements; how exact they have to be, the bound alone decides.
A program may use at most 128 MiB of HBM per device.

v0:
```python
import functools
import math

import jax
import jax.numpy as jnp
import numpy as np
from jax import lax
from jax.experimental import pallas as pl
from jax.experimental.pallas import tpu as pltpu
from jax.sharding import PartitionSpec as P

EPS_SCALE = 0.01
SENSOR_CENTRE = -3.0
SENSOR_WIDTH = 1.5
RATIO_FLOOR = 1e-06
ENERGY_EPS = 1e-06
GAUSS_NODES = [-0.906179845938664, -0.5384693101056831, 0.0, 0.5384693101056831, 0.906179845938664]
GAUSS_WEIGHTS = [
    0.2369268850561891,
    0.4786286704993665,
    0.5688888888888889,
    0.4786286704993665,
    0.2369268850561891,
]


def legendre_values(points):
    values = [np.ones(points.shape), np.array(points)]
    for order in range(1, 5):
        values.append(
            ((2 * order + 1) * points * values[order] - order * values[order - 1]) / (order + 1)
        )
    return values


def line_tables():
    line_nodes = np.array(GAUSS_NODES)
    quadrature_weights = np.array(GAUSS_WEIGHTS)
    barycentric = np.array(
        [
            1.0 / np.prod([line_nodes[j] - line_nodes[k] for k in range(5) if k != j])
            for j in range(5)
        ]
    )
    derivative = np.zeros((5, 5))
    for i in range(5):
        for j in range(5):
            if i != j:
                derivative[i, j] = barycentric[j] / barycentric[i] / (line_nodes[i] - line_nodes[j])
        derivative[i, i] = -np.sum(derivative[i])
    left_values = np.ones(5)
    right_values = np.ones(5)
    for j in range(5):
        for k in range(5):
            if k != j:
                left_values[j] *= (-1.0 - line_nodes[k]) / (line_nodes[j] - line_nodes[k])
                right_values[j] *= (1.0 - line_nodes[k]) / (line_nodes[j] - line_nodes[k])
    legendre = legendre_values(line_nodes)
    fourth_slope = 7.0 * legendre[3] + 3.0 * legendre[1]
    fifth_slope = 9.0 * legendre[4] + 5.0 * legendre[2] + legendre[0]
    left_corr = 0.5 * (fourth_slope - fifth_slope)
    right_corr = 0.5 * (fourth_slope + fifth_slope)
    modal = np.zeros((5, 5))
    for k in range(5):
        modal[k, :] = quadrature_weights * math.sqrt((2 * k + 1) / 2.0) * legendre[k]
    return (line_nodes, derivative, left_values, right_values, left_corr, right_corr, modal)


NODES, DERIV, LEFT, RIGHT, LIFT_LEFT, LIFT_RIGHT, MODAL = line_tables()
HALF_LEFT = 0.5 * LIFT_LEFT
HALF_RIGHT = 0.5 * LIFT_RIGHT


def fold(u):
    return (u[0] + u[4], u[1] + u[3], u[2], u[0] - u[4], u[1] - u[3])


def traces(parts):
    s0, s1, mid, d0, d1 = parts
    r = [float(x) for x in RIGHT]
    even = 0.5 * (r[0] + r[4]) * s0 + 0.5 * (r[1] + r[3]) * s1 + r[2] * mid
    odd = 0.5 * (r[0] - r[4]) * d0 + 0.5 * (r[1] - r[3]) * d1
    return even - odd, even + odd


def slope(parts, jump_left, jump_right):
    s0, s1, mid, d0, d1 = parts
    h = [float(x) for x in HALF_LEFT]
    diff = jump_left - jump_right
    both = jump_left + jump_right
    even, odd = [], []
    for i in range(3):
        even.append(
            float(0.5 * (DERIV[i, 0] - DERIV[i, 4])) * d0
            + float(0.5 * (DERIV[i, 1] - DERIV[i, 3])) * d1
            + 0.5 * (h[i] + h[4 - i]) * diff
        )
    for i in range(2):
        odd.append(
            float(0.5 * (DERIV[i, 0] + DERIV[i, 4])) * s0
            + float(0.5 * (DERIV[i, 1] + DERIV[i, 3])) * s1
            + float(DERIV[i, 2]) * mid
            + 0.5 * (h[i] - h[4 - i]) * both
        )
    return [even[0] + odd[0], even[1] + odd[1], even[2], even[1] - odd[1], even[0] - odd[0]]


def points(axis, q, j):
    if axis == 0:
        return [25 * i + 5 * q + j for i in range(5)]
    if axis == 1:
        return [25 * q + 5 * i + j for i in range(5)]
    return [25 * q + 5 * j + i for i in range(5)]


def modal_line(u):
    s0, s1, mid, d0, d1 = fold(u)
    out = []
    for k in range(5):
        m = [float(x) for x in MODAL[k]]
        out.append(m[0] * s0 + m[1] * s1 + m[2] * mid if k % 2 == 0 else m[0] * d0 + m[1] * d1)
    return out


def sensor(load, work):
    def first(q, carry):
        for j in range(5):
            pts = points(0, q, j)
            for i, value in zip(pts, modal_line([load(p) for p in pts])):
                work[i] = value
        return carry

    lax.fori_loop(0, 5, first, 0)

    def second(q, carry):
        total, high = carry
        plane = {}
        for c in range(5):
            for b, value in enumerate(modal_line([work[25 * q + 5 * b + c] for b in range(5)])):
                plane[b, c] = value
        low = jnp.zeros_like(total)
        edge = jnp.zeros_like(total)
        for b in range(5):
            line = modal_line([plane[b, c] for c in range(5)])
            squares = [x * x for x in line]
            if b < 4:
                low = low + ((squares[0] + squares[1]) + (squares[2] + squares[3]))
                edge = edge + squares[4]
            else:
                edge = edge + ((squares[0] + squares[1]) + (squares[2] + squares[3])) + squares[4]
        plane_total = low + edge
        return total + plane_total, high + jnp.where(q == 4, plane_total, edge)

    zero = jnp.zeros(work.shape[1:], jnp.float32)
    total, high = lax.fori_loop(0, 5, second, (zero, zero))
    level = jnp.log(jnp.maximum(high / (total + ENERGY_EPS), RATIO_FLOOR)) * (1.0 / math.log(10.0))
    ramp = jnp.clip((level - SENSOR_CENTRE) / SENSOR_WIDTH, -1.0, 1.0)
    return EPS_SCALE * 0.5 * (1.0 + jnp.sin(0.5 * math.pi * ramp))


def rolled(value, shift, axis):
    size = value.shape[axis]
    return pltpu.roll(value, shift % size, axis)


def interpolate(neighbours, nu):
    rows, lanes = nu.shape[1:]
    lane = lax.broadcasted_iota(jnp.int32, (rows, lanes), 1)
    corner = {}
    for x in range(2):
        for y in range(2):
            line = jnp.maximum(
                jnp.maximum(neighbours[x][y], neighbours[x + 1][y]),
                jnp.maximum(neighbours[x][y + 1], neighbours[x + 1][y + 1]),
            )
            before = jnp.where(lane == 0, 0.0, rolled(line, 1, 1))
            after = jnp.where(lane == lanes - 1, 0.0, rolled(line, -1, 1))
            corner[x, y, 0] = jnp.maximum(line, before)
            corner[x, y, 1] = jnp.maximum(line, after)
    lower = [float((1.0 - x) / 2.0) for x in NODES]
    upper = [float((1.0 + x) / 2.0) for x in NODES]
    for a in range(5):
        face = {
            (y, z): lower[a] * corner[0, y, z] + upper[a] * corner[1, y, z]
            for y in range(2)
            for z in range(2)
        }
        for b in range(5):
            edge = [lower[b] * face[0, z] + upper[b] * face[1, z] for z in range(2)]
            for c in range(5):
                nu[25 * a + 5 * b + c] = lower[c] * edge[0] + upper[c] * edge[1]


def row_masks(axis, chords, spans, lanes):
    row = lax.broadcasted_iota(jnp.int32, (chords * spans, lanes), 0)
    if axis == 0:
        return row < spans, row >= (chords - 1) * spans
    place = row % spans
    return place == 0, place == spans - 1


def outer_rows(axis, chords, spans, last):
    if axis == 0:
        return pl.ds((chords - 1) * spans if last else 0, spans)
    return pl.ds(spans - 1 if last else 0, chords, spans)


def trace_kernel(chords, spans, state, eps, c_up, c_down, s_up, s_down, work):
    v = pl.program_id(0)

    @pl.when(v == 0)
    def _():
        eps[...] = sensor(lambda p: state[0, p], work)

    for axis, up, down in ((0, c_up, c_down), (1, s_up, s_down)):

        def body(q, carry):
            for j in range(5):
                left, right = traces(fold([state[0, p] for p in points(axis, q, j)]))
                work[2 * j] = left
                work[2 * j + 1] = right
                down[v, 5 * q + j] = work[2 * j, outer_rows(axis, chords, spans, False)]
                up[v, 5 * q + j] = work[2 * j + 1, outer_rows(axis, chords, spans, True)]
            return carry

        lax.fori_loop(0, 5, body, 0)


def flux_kernel(chords, spans, state, around, nu, c_up, c_down, s_up, s_down, work):
    v = pl.program_id(0)
    lanes = nu.shape[-1]

    @pl.when(v == 0)
    def _():
        interpolate([[around[x, y] for y in range(3)] for x in range(3)], nu)

    for axis, up, down in ((0, c_up, c_down), (1, s_up, s_down)):
        low, high = row_masks(axis, chords, spans, lanes)
        step = spans if axis == 0 else 1
        rows_low = outer_rows(axis, chords, spans, False)
        rows_high = outer_rows(axis, chords, spans, True)

        def body(q, carry):
            for j in range(5):
                pts = points(axis, q, j)
                parts = fold([state[0, p] for p in pts])
                left, right = traces(parts)
                before = jnp.where(low, 0.0, rolled(right, step, 0))
                after = jnp.where(high, 0.0, rolled(left, -step, 0))
                gradient = slope(parts, before - left, after - right)
                flux = [nu[p] * g for p, g in zip(pts, gradient)]
                left, right = traces(fold(flux))
                work[2 * j] = left
                work[2 * j + 1] = right
                down[v, 5 * q + j] = work[2 * j, rows_low]
                up[v, 5 * q + j] = work[2 * j + 1, rows_high]
            return carry

        lax.fori_loop(0, 5, body, 0)

        @pl.when(v == 0)
        def _():
            def weights(q, carry):
                for j in range(5):
                    local = [nu[p] for p in points(axis, q, j)]
                    left = sum(float(LEFT[i] * HALF_LEFT[i]) * local[i] for i in range(5))
                    right = sum(float(RIGHT[i] * HALF_RIGHT[i]) * local[i] for i in range(5))
                    work[2 * j] = left
                    work[2 * j + 1] = right
                    down[pl.num_programs(0), 5 * q + j] = work[2 * j, rows_low]
                    up[pl.num_programs(0), 5 * q + j] = work[2 * j + 1, rows_high]
                return carry

            lax.fori_loop(0, 5, weights, 0)


def residual_kernel(
    chords, spans, state, nu, c_up, c_down, s_up, s_down,
    fc_up, fc_down, fs_up, fs_down, out, ghost, alpha, beta,
):
    v = pl.program_id(0)
    count = pl.num_programs(0)
    rows, lanes = nu.shape[1:]
    lane = lax.broadcasted_iota(jnp.int32, (rows, lanes), 1)
    row = lax.broadcasted_iota(jnp.int32, (rows, lanes), 0)
    place = lax.axis_index("chord")
    closed_low = row < jnp.where(place == 0, spans, 0)
    closed_high = row >= jnp.where(place == lax.axis_size("chord") - 1, rows - spans, rows)

    def normal(q, carry):
        first, last = lane == 0, lane == lanes - 1
        for j in range(5):
            pts = points(2, q, j)
            parts = fold([state[0, p] for p in pts])
            left, right = traces(parts)
            jump_left = jnp.where(first, 0.0, rolled(right, 1, 1) - left)
            jump_right = jnp.where(last, 0.0, rolled(left, -1, 1) - right)
            parts = fold([nu[p] * g for p, g in zip(pts, slope(parts, jump_left, jump_right))])
            left, right = traces(parts)
            jump_left = jnp.where(first, -left, rolled(right, 1, 1)) - left
            jump_right = jnp.where(last, -right, rolled(left, -1, 1)) - right
            for p, value in zip(pts, slope(parts, jump_left, jump_right)):
                out[0, p] = value
        return carry

    lax.fori_loop(0, 5, normal, 0)

    for axis, up, down, f_up, f_down in (
        (0, c_up, c_down, fc_up, fc_down),
        (1, s_up, s_down, fs_up, fs_down),
    ):
        low, high = row_masks(axis, chords, spans, lanes)
        step = spans if axis == 0 else 1
        rows_low = outer_rows(axis, chords, spans, False)
        rows_high = outer_rows(axis, chords, spans, True)

        def gather(q, carry):
            for j in range(5):
                f = 5 * q + j
                ghost[f, rows_low] = up[v, f]
                ghost[f, rows_high] = down[v, f]
                alpha[f, rows_low] = f_up[v, f]
                alpha[f, rows_high] = f_down[v, f]
                beta[f, rows_low] = f_up[count, f]
                beta[f, rows_high] = f_down[count, f]
            return carry

        lax.fori_loop(0, 5, gather, 0)

        def body(q, carry):
            for j in range(5):
                f = 5 * q + j
                pts = points(axis, q, j)
                parts = fold([state[0, p] for p in pts])
                left, right = traces(parts)
                outside = ghost[f]
                before = jnp.where(low, outside, rolled(right, step, 0))
                after = jnp.where(high, outside, rolled(left, -step, 0))
                jump_left = before - left
                jump_right = after - right
                if axis == 0:
                    jump_left = jnp.where(closed_low, 0.0, jump_left)
                    jump_right = jnp.where(closed_high, 0.0, jump_right)
                own_left, own_right = left, right
                flux = [nu[p] * g for p, g in zip(pts, slope(parts, jump_left, jump_right))]
                parts = fold(flux)
                left, right = traces(parts)
                a, b = alpha[f], beta[f]
                before = jnp.where(low, a + b * own_left, rolled(right, step, 0))
                after = jnp.where(high, a + b * own_right, rolled(left, -step, 0))
                if axis == 0:
                    before = jnp.where(closed_low, -left, before)
                    after = jnp.where(closed_high, -right, after)
                for p, value in zip(pts, slope(parts, before - left, after - right)):
                    out[0, p] += value
            return carry

        lax.fori_loop(0, 5, body, 0)


def along(block, axis, by):
    devices = lax.axis_size(axis)
    route = [(i, i + by) for i in range(devices)]
    if axis == "span":
        route = [(i, j % devices) for i, j in route]
    else:
        route = [(i, j) for i, j in route if 0 <= j < devices]
    return lax.ppermute(block, axis, route)


def grown(eps):
    for axis, dim in (("span", 1), ("chord", 0)):
        length = eps.shape[dim]
        before = along(lax.slice_in_dim(eps, length - 1, length, axis=dim), axis, 1)
        after = along(lax.slice_in_dim(eps, 0, 1, axis=dim), axis, -1)
        eps = jnp.concatenate([before, eps, after], axis=dim)
    return eps


def shards(state):
    count, npts, chords, spans, lanes = state.shape
    rows = chords * spans
    flat = state.reshape(count, npts, rows, lanes)
    f32 = jnp.float32
    per_variable = pl.BlockSpec((1, npts, rows, lanes), lambda v: (v, 0, 0, 0))

    def whole(*shape):
        return pl.BlockSpec(shape, lambda v: (0,) * len(shape))

    def messages(n):
        shapes = [(n, 25, spans, lanes)] * 2 + [(n, 25, chords, lanes)] * 2
        return [whole(*s) for s in shapes], [jax.ShapeDtypeStruct(s, f32) for s in shapes]

    specs, shapes = messages(count)
    f_specs, f_shapes = messages(count + 1)
    eps, *traced = pl.pallas_call(
        functools.partial(trace_kernel, chords, spans),
        grid=(count,),
        in_specs=[per_variable],
        out_specs=[whole(rows, lanes)] + specs,
        out_shape=[jax.ShapeDtypeStruct((rows, lanes), f32)] + shapes,
        scratch_shapes=[pltpu.VMEM((npts, rows, lanes), f32)],
    )(flat)
    steps = (("chord", 1), ("chord", -1), ("span", 1), ("span", -1))
    wide = grown(eps.reshape(chords, spans, lanes))
    ghosts = [along(m, axis, by) for m, (axis, by) in zip(traced, steps)]
    around = jnp.stack(
        [wide[x : x + chords, y : y + spans] for x in range(3) for y in range(3)]
    ).reshape(3, 3, rows, lanes)
    nu, *fluxes = pl.pallas_call(
        functools.partial(flux_kernel, chords, spans),
        grid=(count,),
        in_specs=[per_variable, whole(3, 3, rows, lanes)],
        out_specs=[whole(npts, rows, lanes)] + f_specs,
        out_shape=[jax.ShapeDtypeStruct((npts, rows, lanes), f32)] + f_shapes,
        scratch_shapes=[pltpu.VMEM((10, rows, lanes), f32)],
    )(flat, around)
    flux_ghosts = [along(m, axis, by) for m, (axis, by) in zip(fluxes, steps)]
    residual = pl.pallas_call(
        functools.partial(residual_kernel, chords, spans),
        grid=(count,),
        in_specs=[per_variable, whole(npts, rows, lanes)] + specs + f_specs,
        out_specs=per_variable,
        out_shape=jax.ShapeDtypeStruct(flat.shape, f32),
        scratch_shapes=[pltpu.VMEM((25, rows, lanes), f32)] * 3,
    )(flat, nu, *ghosts, *flux_ghosts)
    return residual.reshape(state.shape), nu.reshape(npts, chords, spans, lanes)


def solution(mesh):
    in_specs = (P(None, None, "chord", "span", None),)
    out_specs = (P(None, None, "chord", "span", None), P(None, "chord", "span", None))
    return jax.shard_map(shards, mesh=mesh, in_specs=in_specs, out_specs=out_specs, check_vma=False)
```

profile of v0, /device:TPU:0, one launch (start us, length us, event | category | flops | bytes accessed | tf_op | source)
XLA Modules:
  0.0 67.5 jit_solution(6018849270579254211)
XLA Ops:
  0.6 5.1 %shard_map.30 = (f32[8,128]{1,0:T(8,128)}, f32[5,25,2,128]{3,2,1,0:T(2,128)}, f32[5,25,2,128]{3,2,1,0:T(2,128)}, f32[5,25,4,128]{3,2,1,0:T(4,128)}, f32[5,25,4,128]{3,2,1,0:T(4,128)}) custom-call(f32[5,125,8,128]{3,2,1,0:T(8,128)} %bitcast.38), custom_call_target="tpu_custom_call" | custom-call | tf_op jit(solution)/shard_map/pallas_call | solution.py:396
  5.7 0.8 %fusion.2 = (f32[4,1,128]{2,1,0:T(1,128)S(1)}, f32[4,1,128]{2,1,0:T(1,128)S(1)}) fusion(f32[4,2,128]{2,1,0:T(2,128)} %bitcast.43), kind=kLoop, calls=%fused_computation.24 | loop fusion | bytes 8192 | tf_op jit(solution)/shard_map/slice | solution.py:374
  6.5 0.5 collective-permute-start
  7.0 2.9 %collective-permute-start.1 = (f32[4,1,128]{2,1,0:T(1,128)S(1)}, f32[4,1,128]{2,1,0:T(1,128)S(1)}, u32[]{:S(2)}, u32[]{:S(2)}) collective-permute-start(f32[4,1,128]{2,1,0:T(1,128)S(1)} %get-tuple-element.27), channel_id=1, source_target_pairs={{0,7},{1,0},{2,1},{3,2},{4,3},{5,4},{6,5},{7,6},{8,15},{9,8},{10,9... | collective-permute-start | bytes 6152 | tf_op jit(solution)/shard_map/ppermute | solution.py:368
  9.9 1.2 %collective-permute-done = f32[4,1,128]{2,1,0:T(1,128)S(1)} collective-permute-done((f32[4,1,128]{2,1,0:T(1,128)S(1)}, f32[4,1,128]{2,1,0:T(1,128)S(1)}, u32[]{:S(2)}, u32[]{:S(2)}) %collective-permute-start) | collective-permute-done | bytes 2080 | tf_op jit(solution)/shard_map/ppermute | solution.py:368
  11.2 0.7 %pad_maximum_fusion.3 = (f32[1,4,128]{2,1,0:T(4,128)S(1)}, f32[1,4,128]{2,1,0:T(4,128)S(1)}) fusion(f32[4,1,128]{2,1,0:T(1,128)S(1)} %collective-permute-done.1, f32[4,2,128]{2,1,0:T(2,128)} %bitcast.44, f32[4,1,128]{2,1,0:T(1,128)S(1)} %collective-permute-done), kind=kLoop, calls=%fused_computation.21 | loop fusion | flops 2048 | bytes 12288 | tf_op jit(solution)/shard_map/concatenate | solution.py:376
  11.9 1.3 %collective-permute-start.3 = (f32[1,4,128]{2,1,0:T(4,128)S(1)}, f32[1,4,128]{2,1,0:T(4,128)S(1)}, u32[]{:S(2)}, u32[]{:S(2)}) collective-permute-start(f32[1,4,128]{2,1,0:T(4,128)S(1)} %get-tuple-element.24), channel_id=1, source_target_pairs={{8,0},{16,8},{24,16},{9,1},{17,9},{25,17},{10,2},{18,10},{26,18},{... | collective-permute-start | bytes 6152 | tf_op jit(solution)/shard_map/ppermute | solution.py:368
  13.2 4.8 %collective-permute-start.2 = (f32[1,4,128]{2,1,0:T(4,128)S(1)}, f32[1,4,128]{2,1,0:T(4,128)S(1)}, u32[]{:S(2)}, u32[]{:S(2)}) collective-permute-start(f32[1,4,128]{2,1,0:T(4,128)S(1)} %get-tuple-element.25), channel_id=1, source_target_pairs={{0,8},{8,16},{16,24},{1,9},{9,17},{17,25},{2,10},{10,18},{18,26},{... | collective-permute-start | bytes 6152 | tf_op jit(solution)/shard_map/ppermute | solution.py:368
  18.0 3.9 %collective-permute-start.4 = (f32[5,25,2,128]{3,2,1,0:T(2,128)}, f32[5,25,2,128]{3,2,1,0:T(2,128)S(1)}, u32[]{:S(2)}, u32[]{:S(2)}) collective-permute-start(f32[5,25,2,128]{3,2,1,0:T(2,128)} %get-tuple-element.14), channel_id=1, source_target_pairs={{0,8},{8,16},{16,24},{1,9},{9,17},{17,25},{2,10},{10,18},{18,26},{... | collective-permute-start | bytes 384008 | tf_op jit(solution)/shard_map/ppermute | solution.py:368
  22.0 1.3 %collective-permute-start.5 = (f32[5,25,2,128]{3,2,1,0:T(2,128)}, f32[5,25,2,128]{3,2,1,0:T(2,128)S(1)}, u32[]{:S(2)}, u32[]{:S(2)}) collective-permute-start(f32[5,25,2,128]{3,2,1,0:T(2,128)} %get-tuple-element.15), channel_id=1, source_target_pairs={{8,0},{16,8},{24,16},{9,1},{17,9},{25,17},{10,2},{18,10},{26,18},{... | collective-permute-start | bytes 384008 | tf_op jit(solution)/shard_map/ppermute | solution.py:368
  23.3 0.8 %pad_maximum_fusion = (f32[5,4,128]{2,1,0:T(4,128)S(1)}, f32[5,4,128]{2,1,0:T(4,128)S(1)}) fusion(f32[1,4,128]{2,1,0:T(4,128)S(1)} %collective-permute-done.3, f32[4,1,128]{2,1,0:T(1,128)S(1)} %collective-permute-done.1, f32[4,2,128]{2,1,0:T(2,128)} %bitcast.45, f32[4,1,128]{2,1,0:T(1,128)S(1)} %collective-permute-done, ...), kind=kLoop, calls=%fused_computation.10 | loop fusion | flops 15360 | bytes 32768 | tf_op jit(solution)/shard_map/concatenate | solution.py:376
  24.1 0.7 %constant_dynamic-update-slice_fusion.5 = f32[9,4,2,128]{3,2,1,0:T(2,128)S(1)} fusion(f32[9,4,2,128]{3,2,1,0:T(2,128)S(1)} %constant_dynamic-update-slice_fusion.6, f32[4,2,128]{2,1,0:T(2,128)} %bitcast.46, f32[4,1,128]{2,1,0:T(1,128)S(1)} %collective-permute-done), kind=kLoop, calls=%fused_computation.5 | loop fusion | flops 1024 | bytes 10240
  24.8 0.7 %constant_dynamic-update-slice_fusion.4 = f32[9,4,2,128]{3,2,1,0:T(2,128)S(1)} fusion(f32[9,4,2,128]{3,2,1,0:T(2,128)S(1)} %constant_dynamic-update-slice_fusion.5, f32[1,4,2,128]{3,2,1,0:T(2,128)} %bitcast.47), kind=kLoop, calls=%fused_computation.4 | loop fusion | bytes 8192
  25.5 0.7 %constant_dynamic-update-slice_fusion.3 = f32[9,4,2,128]{3,2,1,0:T(2,128)S(1)} fusion(f32[9,4,2,128]{3,2,1,0:T(2,128)S(1)} %constant_dynamic-update-slice_fusion.4, f32[4,1,128]{2,1,0:T(1,128)S(1)} %collective-permute-done.1, f32[4,2,128]{2,1,0:T(2,128)} %bitcast.48), kind=kLoop, calls=%fused_computation.3 | loop fusion | flops 1024 | bytes 10240
  26.3 0.6 copy-done.8
  26.9 6.8 %shard_map.31 = (f32[125,8,128]{2,1,0:T(8,128)}, f32[6,25,2,128]{3,2,1,0:T(2,128)}, f32[6,25,2,128]{3,2,1,0:T(2,128)}, f32[6,25,4,128]{3,2,1,0:T(4,128)}, f32[6,25,4,128]{3,2,1,0:T(4,128)}) custom-call(f32[5,125,8,128]{3,2,1,0:T(8,128)} %bitcast.39, f32[3,3,8,128]{3,2,1,0:T(8,128)} %bitcast.49), custom_call_target="tpu_custom_call" | custom-call | tf_op jit(solution)/shard_map/pallas_call | solution.py:410
  33.7 4.5 %collective-permute-start.8 = (f32[6,25,2,128]{3,2,1,0:T(2,128)}, f32[6,25,2,128]{3,2,1,0:T(2,128)S(1)}, u32[]{:S(2)}, u32[]{:S(2)}) collective-permute-start(f32[6,25,2,128]{3,2,1,0:T(2,128)} %get-tuple-element.18), channel_id=1, source_target_pairs={{0,8},{8,16},{16,24},{1,9},{9,17},{17,25},{2,10},{10,18},{18,26},{... | collective-permute-start | bytes 460808 | tf_op jit(solution)/shard_map/ppermute | solution.py:368
  38.3 2.6 %collective-permute-start.11 = (f32[6,25,4,128]{3,2,1,0:T(4,128)}, f32[6,25,4,128]{3,2,1,0:T(4,128)S(1)}, u32[]{:S(2)}, u32[]{:S(2)}) collective-permute-start(f32[6,25,4,128]{3,2,1,0:T(4,128)} %get-tuple-element.21), channel_id=1, source_target_pairs={{0,7},{1,0},{2,1},{3,2},{4,3},{5,4},{6,5},{7,6},{8,15},{9,8},{10,9... | collective-permute-start | bytes 921608 | tf_op jit(solution)/shard_map/ppermute | solution.py:368
  41.0 2.7 %collective-permute-start.7 = (f32[5,25,4,128]{3,2,1,0:T(4,128)S(1)}, f32[5,25,4,128]{3,2,1,0:T(4,128)S(1)}, u32[]{:S(2)}, u32[]{:S(2)}) collective-permute-start(f32[5,25,4,128]{3,2,1,0:T(4,128)S(1)} %copy-done.9), channel_id=1, source_target_pairs={{0,7},{1,0},{2,1},{3,2},{4,3},{5,4},{6,5},{7,6},{8,15},{9,8},{10,9... | collective-permute-start | bytes 768008 | tf_op jit(solution)/shard_map/ppermute | solution.py:368
  43.7 1.3 %collective-permute-start.9 = (f32[6,25,2,128]{3,2,1,0:T(2,128)}, f32[6,25,2,128]{3,2,1,0:T(2,128)S(1)}, u32[]{:S(2)}, u32[]{:S(2)}) collective-permute-start(f32[6,25,2,128]{3,2,1,0:T(2,128)} %get-tuple-element.19), channel_id=1, source_target_pairs={{8,0},{16,8},{24,16},{9,1},{17,9},{25,17},{10,2},{18,10},{26,18},{... | collective-permute-start | bytes 460808 | tf_op jit(solution)/shard_map/ppermute | solution.py:368
  45.0 6.0 %collective-permute-done.9.fc_down = f32[6,25,2,128]{3,2,1,0:T(2,128)S(1)} collective-permute-done((f32[6,25,2,128]{3,2,1,0:T(2,128)}, f32[6,25,2,128]{3,2,1,0:T(2,128)S(1)}, u32[]{:S(2)}, u32[]{:S(2)}) %collective-permute-start.9) | collective-permute-done | bytes 153632 | tf_op jit(solution)/shard_map/ppermute | solution.py:368
  51.0 2.5 %collective-permute-done.6.s_up = f32[5,25,4,128]{3,2,1,0:T(4,128)S(1)} collective-permute-done((f32[5,25,4,128]{3,2,1,0:T(4,128)S(1)}, f32[5,25,4,128]{3,2,1,0:T(4,128)S(1)}, u32[]{:S(2)}, u32[]{:S(2)}) %collective-permute-start.6) | collective-permute-done | bytes 256032 | tf_op jit(solution)/shard_map/ppermute | solution.py:368
  53.6 0.6 copy-done.2
  54.5 13.0 %shard_map.32 = f32[5,125,8,128]{3,2,1,0:T(8,128)} custom-call(f32[5,125,8,128]{3,2,1,0:T(8,128)} %bitcast.40, f32[125,8,128]{2,1,0:T(8,128)} %get-tuple-element.13.nu, f32[5,25,2,128]{3,2,1,0:T(2,128)} %copy-done.6, f32[5,25,2,128]{3,2,1,0:T(2,128)} %copy-done.7, f32[5,25,4,128]{3,2,1,0:T(4,128)} %copy-done.2, f32[5,25,4,128]{3,2,1,0:T(4,128)} %copy-done.3, ...), custom_call_target="tpu_custom_call" | custom-call | tf_op jit(solution)/shard_map/pallas_call | solution.py:419
  (37 shorter events, 0.6 us)
Async XLA Ops:
  5.7 35.2 %copy-start.10 = (f32[5,25,4,128]{3,2,1,0:T(4,128)S(1)}, f32[5,25,4,128]{3,2,1,0:T(4,128)}, u32[]{:S(2)}) copy-start(f32[5,25,4,128]{3,2,1,0:T(4,128)} %get-tuple-element.16) | copy-start | bytes 768004
  5.7 35.3 %copy-start.9 = (f32[5,25,4,128]{3,2,1,0:T(4,128)S(1)}, f32[5,25,4,128]{3,2,1,0:T(4,128)}, u32[]{:S(2)}) copy-start(f32[5,25,4,128]{3,2,1,0:T(4,128)} %get-tuple-element.17) | copy-start | bytes 768004
  6.5 4.6 %collective-permute-start = (f32[4,1,128]{2,1,0:T(1,128)S(1)}, f32[4,1,128]{2,1,0:T(1,128)S(1)}, u32[]{:S(2)}, u32[]{:S(2)}) collective-permute-start(f32[4,1,128]{2,1,0:T(1,128)S(1)} %get-tuple-element.26), channel_id=1, source_target_pairs={{0,1},{1,2},{2,3},{3,4},{4,5},{5,6},{6,7},{7,0},{8,9},{9,10},{10,1... | collective-permute-start | bytes 6152 | tf_op jit(solution)/shard_map/ppermute | solution.py:368
  7.0 4.2 %collective-permute-start.1 = (f32[4,1,128]{2,1,0:T(1,128)S(1)}, f32[4,1,128]{2,1,0:T(1,128)S(1)}, u32[]{:S(2)}, u32[]{:S(2)}) collective-permute-start(f32[4,1,128]{2,1,0:T(1,128)S(1)} %get-tuple-element.27), channel_id=1, source_target_pairs={{0,7},{1,0},{2,1},{3,2},{4,3},{5,4},{6,5},{7,6},{8,15},{9,8},{10,9... | collective-permute-start | bytes 6152 | tf_op jit(solution)/shard_map/ppermute | solution.py:368
  11.9 11.4 %collective-permute-start.3 = (f32[1,4,128]{2,1,0:T(4,128)S(1)}, f32[1,4,128]{2,1,0:T(4,128)S(1)}, u32[]{:S(2)}, u32[]{:S(2)}) collective-permute-start(f32[1,4,128]{2,1,0:T(4,128)S(1)} %get-tuple-element.24), channel_id=1, source_target_pairs={{8,0},{16,8},{24,16},{9,1},{17,9},{25,17},{10,2},{18,10},{26,18},{... | collective-permute-start | bytes 6152 | tf_op jit(solution)/shard_map/ppermute | solution.py:368
  13.2 10.1 %collective-permute-start.2 = (f32[1,4,128]{2,1,0:T(4,128)S(1)}, f32[1,4,128]{2,1,0:T(4,128)S(1)}, u32[]{:S(2)}, u32[]{:S(2)}) collective-permute-start(f32[1,4,128]{2,1,0:T(4,128)S(1)} %get-tuple-element.25), channel_id=1, source_target_pairs={{0,8},{8,16},{16,24},{1,9},{9,17},{17,25},{2,10},{10,18},{18,26},{... | collective-permute-start | bytes 6152 | tf_op jit(solution)/shard_map/ppermute | solution.py:368
  18.0 22.9 %collective-permute-start.4 = (f32[5,25,2,128]{3,2,1,0:T(2,128)}, f32[5,25,2,128]{3,2,1,0:T(2,128)S(1)}, u32[]{:S(2)}, u32[]{:S(2)}) collective-permute-start(f32[5,25,2,128]{3,2,1,0:T(2,128)} %get-tuple-element.14), channel_id=1, source_target_pairs={{0,8},{8,16},{16,24},{1,9},{9,17},{17,25},{2,10},{10,18},{18,26},{... | collective-permute-start | bytes 384008 | tf_op jit(solution)/shard_map/ppermute | solution.py:368
  22.0 19.0 %collective-permute-start.5 = (f32[5,25,2,128]{3,2,1,0:T(2,128)}, f32[5,25,2,128]{3,2,1,0:T(2,128)S(1)}, u32[]{:S(2)}, u32[]{:S(2)}) collective-permute-start(f32[5,25,2,128]{3,2,1,0:T(2,128)} %get-tuple-element.15), channel_id=1, source_target_pairs={{8,0},{16,8},{24,16},{9,1},{17,9},{25,17},{10,2},{18,10},{26,18},{... | collective-permute-start | bytes 384008 | tf_op jit(solution)/shard_map/ppermute | solution.py:368
  26.3 0.6 copy-start.8
  33.7 10.0 %collective-permute-start.8 = (f32[6,25,2,128]{3,2,1,0:T(2,128)}, f32[6,25,2,128]{3,2,1,0:T(2,128)S(1)}, u32[]{:S(2)}, u32[]{:S(2)}) collective-permute-start(f32[6,25,2,128]{3,2,1,0:T(2,128)} %get-tuple-element.18), channel_id=1, source_target_pairs={{0,8},{8,16},{16,24},{1,9},{9,17},{17,25},{2,10},{10,18},{18,26},{... | collective-permute-start | bytes 460808 | tf_op jit(solution)/shard_map/ppermute | solution.py:368
  38.2 15.3 %collective-permute-start.10 = (f32[6,25,4,128]{3,2,1,0:T(4,128)}, f32[6,25,4,128]{3,2,1,0:T(4,128)S(1)}, u32[]{:S(2)}, u32[]{:S(2)}) collective-permute-start(f32[6,25,4,128]{3,2,1,0:T(4,128)} %get-tuple-element.20), channel_id=1, source_target_pairs={{0,1},{1,2},{2,3},{3,4},{4,5},{5,6},{6,7},{7,0},{8,9},{9,10},{10,1... | collective-permute-start | bytes 921608 | tf_op jit(solution)/shard_map/ppermute | solution.py:368
  38.3 15.2 %collective-permute-start.11 = (f32[6,25,4,128]{3,2,1,0:T(4,128)}, f32[6,25,4,128]{3,2,1,0:T(4,128)S(1)}, u32[]{:S(2)}, u32[]{:S(2)}) collective-permute-start(f32[6,25,4,128]{3,2,1,0:T(4,128)} %get-tuple-element.21), channel_id=1, source_target_pairs={{0,7},{1,0},{2,1},{3,2},{4,3},{5,4},{6,5},{7,6},{8,15},{9,8},{10,9... | collective-permute-start | bytes 921608 | tf_op jit(solution)/shard_map/ppermute | solution.py:368
  40.9 12.6 %copy-start.6 = (f32[5,25,2,128]{3,2,1,0:T(2,128)}, f32[5,25,2,128]{3,2,1,0:T(2,128)S(1)}, u32[]{:S(2)}) copy-start(f32[5,25,2,128]{3,2,1,0:T(2,128)S(1)} %collective-permute-done.4.c_up) | copy-start | bytes 384004
  40.9 12.6 %collective-permute-start.6 = (f32[5,25,4,128]{3,2,1,0:T(4,128)S(1)}, f32[5,25,4,128]{3,2,1,0:T(4,128)S(1)}, u32[]{:S(2)}, u32[]{:S(2)}) collective-permute-start(f32[5,25,4,128]{3,2,1,0:T(4,128)S(1)} %copy-done.10), channel_id=1, source_target_pairs={{0,1},{1,2},{2,3},{3,4},{4,5},{5,6},{6,7},{7,0},{8,9},{9,10},{10,1... | collective-permute-start | bytes 768008 | tf_op jit(solution)/shard_map/ppermute | solution.py:368
  41.0 12.6 %copy-start.7 = (f32[5,25,2,128]{3,2,1,0:T(2,128)}, f32[5,25,2,128]{3,2,1,0:T(2,128)S(1)}, u32[]{:S(2)}) copy-start(f32[5,25,2,128]{3,2,1,0:T(2,128)S(1)} %collective-permute-done.5.c_down) | copy-start | bytes 384004
  41.0 12.5 %collective-permute-start.7 = (f32[5,25,4,128]{3,2,1,0:T(4,128)S(1)}, f32[5,25,4,128]{3,2,1,0:T(4,128)S(1)}, u32[]{:S(2)}, u32[]{:S(2)}) collective-permute-start(f32[5,25,4,128]{3,2,1,0:T(4,128)S(1)} %copy-done.9), channel_id=1, source_target_pairs={{0,7},{1,0},{2,1},{3,2},{4,3},{5,4},{6,5},{7,6},{8,15},{9,8},{10,9... | collective-permute-start | bytes 768008 | tf_op jit(solution)/shard_map/ppermute | solution.py:368
  43.7 9.9 %copy-start.4 = (f32[6,25,2,128]{3,2,1,0:T(2,128)}, f32[6,25,2,128]{3,2,1,0:T(2,128)S(1)}, u32[]{:S(2)}) copy-start(f32[6,25,2,128]{3,2,1,0:T(2,128)S(1)} %collective-permute-done.8.fc_up) | copy-start | bytes 460804
  43.7 7.3 %collective-permute-start.9 = (f32[6,25,2,128]{3,2,1,0:T(2,128)}, f32[6,25,2,128]{3,2,1,0:T(2,128)S(1)}, u32[]{:S(2)}, u32[]{:S(2)}) collective-permute-start(f32[6,25,2,128]{3,2,1,0:T(2,128)} %get-tuple-element.19), channel_id=1, source_target_pairs={{8,0},{16,8},{24,16},{9,1},{17,9},{25,17},{10,2},{18,10},{26,18},{... | collective-permute-start | bytes 460808 | tf_op jit(solution)/shard_map/ppermute | solution.py:368
  51.0 2.6 %copy-start.5 = (f32[6,25,2,128]{3,2,1,0:T(2,128)}, f32[6,25,2,128]{3,2,1,0:T(2,128)S(1)}, u32[]{:S(2)}) copy-start(f32[6,25,2,128]{3,2,1,0:T(2,128)S(1)} %collective-permute-done.9.fc_down) | copy-start | bytes 460804
  53.5 0.7 %copy-start.2 = (f32[5,25,4,128]{3,2,1,0:T(4,128)}, f32[5,25,4,128]{3,2,1,0:T(4,128)S(1)}, u32[]{:S(2)}) copy-start(f32[5,25,4,128]{3,2,1,0:T(4,128)S(1)} %collective-permute-done.6.s_up) | copy-start | bytes 768004
  53.5 0.8 %copy-start.3 = (f32[5,25,4,128]{3,2,1,0:T(4,128)}, f32[5,25,4,128]{3,2,1,0:T(4,128)S(1)}, u32[]{:S(2)}) copy-start(f32[5,25,4,128]{3,2,1,0:T(4,128)S(1)} %collective-permute-done.7.s_down) | copy-start | bytes 768004
  53.5 0.9 %copy-start = (f32[6,25,4,128]{3,2,1,0:T(4,128)}, f32[6,25,4,128]{3,2,1,0:T(4,128)S(1)}, u32[]{:S(2)}) copy-start(f32[6,25,4,128]{3,2,1,0:T(4,128)S(1)} %collective-permute-done.10.fs_up) | copy-start | bytes 921604
  53.5 1.0 %copy-start.1 = (f32[6,25,4,128]{3,2,1,0:T(4,128)}, f32[6,25,4,128]{3,2,1,0:T(4,128)S(1)}, u32[]{:S(2)}) copy-start(f32[6,25,4,128]{3,2,1,0:T(4,128)S(1)} %collective-permute-done.11.fs_down) | copy-start | bytes 921604
where the time goes:
time: 68.2 us; the launch traced here: 67.5 us
  starting transfers between devices  26 us (38%)
  Pallas kernels  24.9 us (37%)
  waiting for transfers between devices  9.85 us (14%)
  local copies, waits for them, and re-layouts  3.08 us (5%)
  other arithmetic  2.89 us (4%)
  between operations  0.84 us (1%)
    ppermute x12, starting transfers between devices, along(): return lax.ppermute(block, axis, route)  26 us
    pallas_call x1, Pallas kernels, shards(): pl.pallas_call(functools.partial(residual_kernel, chords, spans), grid=(c...  13 us
    ppermute x12, waiting for transfers between devices, along(): return lax.ppermute(block, axis, route)  9.85 us
    pallas_call x1, Pallas kernels, shards(): pl.pallas_call(functools.partial(flux_kernel, chords, spans), grid=(count...  6.82 us
    pallas_call x1, Pallas kernels, shards(): pl.pallas_call(functools.partial(trace_kernel, chords, spans), grid=(coun...  5.1 us
    unnamed x28, local copies, waits for them, and re-layouts  2.3 us
    concatenate x2, other arithmetic, grown(): eps = jnp.concatenate([before, eps, after], axis=dim)  1.48 us
    unnamed x2, other arithmetic  1.4 us
  transfers between devices with their start and end apart: 12, of which 4 were waited for; matrix products, arithmetic and copies ran while one was open for 4% of the time, Pallas kernels for 10%

commit v1 on v0

v1 whole, which is shorter than its diff:
```python
import functools
import math

import jax
import jax.numpy as jnp
import numpy as np
from jax import lax
from jax.experimental import pallas as pl
from jax.experimental.pallas import tpu as pltpu
from jax.sharding import PartitionSpec as P

EPS_SCALE = 0.01
SENSOR_CENTRE = -3.0
SENSOR_WIDTH = 1.5
RATIO_FLOOR = 1e-06
ENERGY_EPS = 1e-06
GAUSS_NODES = [-0.906179845938664, -0.5384693101056831, 0.0, 0.5384693101056831, 0.906179845938664]
GAUSS_WEIGHTS = [
    0.2369268850561891,
    0.4786286704993665,
    0.5688888888888889,
    0.4786286704993665,
    0.2369268850561891,
]


def legendre_values(points):
    values = [np.ones(points.shape), np.array(points)]
    for order in range(1, 5):
        values.append(
            ((2 * order + 1) * points * values[order] - order * values[order - 1]) / (order + 1)
        )
    return values


def line_tables():
    line_nodes = np.array(GAUSS_NODES)
    quadrature_weights = np.array(GAUSS_WEIGHTS)
    barycentric = np.array(
        [
            1.0 / np.prod([line_nodes[j] - line_nodes[k] for k in range(5) if k != j])
            for j in range(5)
        ]
    )
    derivative = np.zeros((5, 5))
    for i in range(5):
        for j in range(5):
            if i != j:
                derivative[i, j] = barycentric[j] / barycentric[i] / (line_nodes[i] - line_nodes[j])
        derivative[i, i] = -np.sum(derivative[i])
    left_values = np.ones(5)
    right_values = np.ones(5)
    for j in range(5):
        for k in range(5):
            if k != j:
                left_values[j] *= (-1.0 - line_nodes[k]) / (line_nodes[j] - line_nodes[k])
                right_values[j] *= (1.0 - line_nodes[k]) / (line_nodes[j] - line_nodes[k])
    legendre = legendre_values(line_nodes)
    fourth_slope = 7.0 * legendre[3] + 3.0 * legendre[1]
    fifth_slope = 9.0 * legendre[4] + 5.0 * legendre[2] + legendre[0]
    left_corr = 0.5 * (fourth_slope - fifth_slope)
    right_corr = 0.5 * (fourth_slope + fifth_slope)
    modal = np.zeros((5, 5))
    for k in range(5):
        modal[k, :] = quadrature_weights * math.sqrt((2 * k + 1) / 2.0) * legendre[k]
    return (line_nodes, derivative, left_values, right_values, left_corr, right_corr, modal)


NODES, DERIV, LEFT, RIGHT, LIFT_LEFT, LIFT_RIGHT, MODAL = line_tables()
HALF_LEFT = 0.5 * LIFT_LEFT
HALF_RIGHT = 0.5 * LIFT_RIGHT


def fold(u):
    return (u[0] + u[4], u[1] + u[3], u[2], u[0] - u[4], u[1] - u[3])


def traces(parts):
    s0, s1, mid, d0, d1 = parts
    r = [float(x) for x in RIGHT]
    even = 0.5 * (r[0] + r[4]) * s0 + 0.5 * (r[1] + r[3]) * s1 + r[2] * mid
    odd = 0.5 * (r[0] - r[4]) * d0 + 0.5 * (r[1] - r[3]) * d1
    return even - odd, even + odd


def slope(parts, jump_left, jump_right):
    s0, s1, mid, d0, d1 = parts
    h = [float(x) for x in HALF_LEFT]
    diff = jump_left - jump_right
    both = jump_left + jump_right
    even, odd = [], []
    for i in range(3):
        even.append(
            float(0.5 * (DERIV[i, 0] - DERIV[i, 4])) * d0
            + float(0.5 * (DERIV[i, 1] - DERIV[i, 3])) * d1
            + 0.5 * (h[i] + h[4 - i]) * diff
        )
    for i in range(2):
        odd.append(
            float(0.5 * (DERIV[i, 0] + DERIV[i, 4])) * s0
            + float(0.5 * (DERIV[i, 1] + DERIV[i, 3])) * s1
            + float(DERIV[i, 2]) * mid
            + 0.5 * (h[i] - h[4 - i]) * both
        )
    return [even[0] + odd[0], even[1] + odd[1], even[2], even[1] - odd[1], even[0] - odd[0]]


def points(axis, q, j):
    if axis == 0:
        return [25 * i + 5 * q + j for i in range(5)]
    if axis == 1:
        return [25 * q + 5 * i + j for i in range(5)]
    return [25 * q + 5 * j + i for i in range(5)]


def modal_line(u):
    s0, s1, mid, d0, d1 = fold(u)
    out = []
    for k in range(5):
        m = [float(x) for x in MODAL[k]]
        out.append(m[0] * s0 + m[1] * s1 + m[2] * mid if k % 2 == 0 else m[0] * d0 + m[1] * d1)
    return out


def sensor(load, work):
    def first(q, carry):
        for j in range(5):
            pts = points(0, q, j)
            for i, value in zip(pts, modal_line([load(p) for p in pts])):
                work[i] = value
        return carry

    lax.fori_loop(0, 5, first, 0)

    def second(q, carry):
        total, high = carry
        plane = {}
        for c in range(5):
            for b, value in enumerate(modal_line([work[25 * q + 5 * b + c] for b in range(5)])):
                plane[b, c] = value
        low = jnp.zeros_like(total)
        edge = jnp.zeros_like(total)
        for b in range(5):
            line = modal_line([plane[b, c] for c in range(5)])
            squares = [x * x for x in line]
            if b < 4:
                low = low + ((squares[0] + squares[1]) + (squares[2] + squares[3]))
                edge = edge + squares[4]
            else:
                edge = edge + ((squares[0] + squares[1]) + (squares[2] + squares[3])) + squares[4]
        plane_total = low + edge
        return total + plane_total, high + jnp.where(q == 4, plane_total, edge)

    zero = jnp.zeros(work.shape[1:], jnp.float32)
    total, high = lax.fori_loop(0, 5, second, (zero, zero))
    level = jnp.log(jnp.maximum(high / (total + ENERGY_EPS), RATIO_FLOOR)) * (1.0 / math.log(10.0))
    ramp = jnp.clip((level - SENSOR_CENTRE) / SENSOR_WIDTH, -1.0, 1.0)
    return EPS_SCALE * 0.5 * (1.0 + jnp.sin(0.5 * math.pi * ramp))


def rolled(value, shift, axis):
    size = value.shape[axis]
    return pltpu.roll(value, shift % size, axis)


def interpolate(neighbours, nu):
    rows, lanes = nu.shape[1:]
    lane = lax.broadcasted_iota(jnp.int32, (rows, lanes), 1)
    corner = {}
    for x in range(2):
        for y in range(2):
            line = jnp.maximum(
                jnp.maximum(neighbours[x][y], neighbours[x + 1][y]),
                jnp.maximum(neighbours[x][y + 1], neighbours[x + 1][y + 1]),
            )
            before = jnp.where(lane == 0, 0.0, rolled(line, 1, 1))
            after = jnp.where(lane == lanes - 1, 0.0, rolled(line, -1, 1))
            corner[x, y, 0] = jnp.maximum(line, before)
            corner[x, y, 1] = jnp.maximum(line, after)
    lower = [float((1.0 - x) / 2.0) for x in NODES]
    upper = [float((1.0 + x) / 2.0) for x in NODES]
    for a in range(5):
        face = {
            (y, z): lower[a] * corner[0, y, z] + upper[a] * corner[1, y, z]
            for y in range(2)
            for z in range(2)
        }
        for b in range(5):
            edge = [lower[b] * face[0, z] + upper[b] * face[1, z] for z in range(2)]
            for c in range(5):
                nu[25 * a + 5 * b + c] = lower[c] * edge[0] + upper[c] * edge[1]


def row_masks(axis, chords, spans, lanes):
    row = lax.broadcasted_iota(jnp.int32, (chords * spans, lanes), 0)
    if axis == 0:
        return row < spans, row >= (chords - 1) * spans
    place = row % spans
    return place == 0, place == spans - 1


def outer_rows(axis, chords, spans, last):
    if axis == 0:
        return pl.ds((chords - 1) * spans if last else 0, spans)
    return pl.ds(spans - 1 if last else 0, chords, spans)


def store_pair(work, slot, left, right, down, up, index, rows_low, rows_high):
    work[2 * slot] = left
    work[2 * slot + 1] = right
    down[index] = work[2 * slot, rows_low]
    up[index] = work[2 * slot + 1, rows_high]


def local_kernel(sizes, count, chords, spans, *refs):
    state_hbm = refs[0]
    nu, faces_c, faces_s, partial = refs[1:5]
    ghosts = refs[5:9]
    flux_ghosts = refs[9:13]
    (
        state, acc, around, work, eps_out,
        t0, t1, t2, t3, f0, f1, f2, f3,
        load_sem, store_sem, eps_send, eps_recv, send_sem, recv_sem,
    ) = refs[13:]
    sends = ((t0, t1, t2, t3), (f0, f1, f2, f3))
    lands = (ghosts, flux_ghosts)
    rows, lanes = nu.shape[1:]
    chord_size, span_size = sizes
    me_c, me_s = lax.axis_index("chord"), lax.axis_index("span")
    mesh_id = pl.DeviceIdType.MESH

    def load(v):
        return pltpu.make_async_copy(state_hbm.at[v], state.at[v], load_sem.at[v])

    for v in range(count):
        load(v).start()

    def reachable(dx):
        if dx == 0:
            return None
        return me_c + 1 < chord_size if dx == 1 else me_c > 0

    def guarded(cond, run):
        if cond is None:
            run()
        else:
            pl.when(cond)(run)

    def partner(dx, dy):
        return (me_c + dx, lax.rem(me_s + dy + span_size, span_size))

    offsets = [(dx, dy) for dx in (0, -1, 1) for dy in (-1, 0, 1) if (dx, dy) != (0, 0)]
    barrier = pltpu.get_barrier_semaphore()
    for dx, dy in offsets:

        def greet(dx=dx, dy=dy):
            pl.semaphore_signal(barrier, inc=1, device_id=partner(dx, dy), device_id_type=mesh_id)

        guarded(reachable(dx), greet)

    load(0).wait()
    eps = sensor(lambda p: state[0, p], work)
    eps_out[...] = eps
    around[1, 1] = eps
    sides = jnp.where(me_c > 0, 1, 0) + jnp.where(me_c + 1 < chord_size, 1, 0)
    pl.semaphore_wait(barrier, 2 + 3 * sides)

    def eps_copy(dx, dy):
        slot = 3 * (dx + 1) + dy + 1
        return pltpu.make_async_remote_copy(
            src_ref=eps_out, dst_ref=around.at[1 - dx, 1 - dy],
            send_sem=eps_send.at[slot], recv_sem=eps_recv.at[8 - slot],
            device_id=partner(dx, dy), device_id_type=mesh_id,
        )

    for dx, dy in offsets:
        guarded(reachable(dx), lambda dx=dx, dy=dy: eps_copy(dx, dy).start())

    ways = ((1, 0), (-1, 0), (0, 1), (0, -1))

    def message(stage, k, v):
        dx, dy = ways[k]
        return pltpu.make_async_remote_copy(
            src_ref=sends[stage][k].at[v], dst_ref=lands[stage][k].at[v],
            send_sem=send_sem.at[stage, k, v], recv_sem=recv_sem.at[stage, k, v],
            device_id=partner(dx, dy), device_id_type=mesh_id,
        )

    def launch(stage, axis, v):
        for k in (2 * axis, 2 * axis + 1):
            guarded(reachable(ways[k][0]), lambda k=k: message(stage, k, v).start())

    masks = [row_masks(axis, chords, spans, lanes) for axis in range(2)]
    outer = [[outer_rows(axis, chords, spans, last) for last in (False, True)] for axis in range(2)]

    def send_traces(v, carry):
        @pl.when(v > 0)
        def _():
            load(v).wait()

        for axis in (1, 0):
            up, down = sends[0][2 * axis], sends[0][2 * axis + 1]
            faces = (faces_c, faces_s)[axis]

            def body(q, carry):
                for j in range(5):
                    left, right = traces(fold([state[v, p] for p in points(axis, q, j)]))
                    faces[v, 5 * q + j] = jnp.where(masks[axis][0], left, right)
                    store_pair(work, j, left, right, down, up, (v, 5 * q + j), *outer[axis])
                return carry

            lax.fori_loop(0, 5, body, 0)
            launch(0, axis, v)
        return carry

    lax.fori_loop(0, count, send_traces, 0)

    row = lax.broadcasted_iota(jnp.int32, (rows, lanes), 0)
    for dx, dy in offsets:
        guarded(reachable(-dx), lambda dx=dx, dy=dy: eps_copy(dx, dy).wait_recv())

    have_low = jnp.where(me_c > 0, spans, 0)
    have_high = jnp.where(me_c + 1 < chord_size, rows, rows - spans)
    column = []
    for x in range(3):
        mine, left, right = around[x, 1], around[x, 0], around[x, 2]
        column.append([
            jnp.where(masks[1][0], rolled(left, 1 - spans, 0), rolled(mine, 1, 0)),
            mine,
            jnp.where(masks[1][1], rolled(right, spans - 1, 0), rolled(mine, -1, 0)),
        ])
    neighbours = [[], [], []]
    for y in range(3):
        inner = column[1][y]
        below = jnp.where(masks[0][0], rolled(column[0][y], spans, 0), rolled(inner, spans, 0))
        above = jnp.where(masks[0][1], rolled(column[2][y], -spans, 0), rolled(inner, -spans, 0))
        neighbours[0].append(jnp.where(row < spans - have_low, 0.0, below))
        neighbours[1].append(inner)
        neighbours[2].append(jnp.where(row >= have_high, 0.0, above))
    interpolate(neighbours, nu)

    closed_low = row < spans - have_low
    closed_high = row >= have_high

    for axis in (1, 0):
        up, down = sends[1][2 * axis], sends[1][2 * axis + 1]

        def weights(q, carry):
            for j in range(5):
                local = [nu[p] for p in points(axis, q, j)]
                left = sum(float(LEFT[i] * HALF_LEFT[i]) * local[i] for i in range(5))
                right = sum(float(RIGHT[i] * HALF_RIGHT[i]) * local[i] for i in range(5))
                store_pair(work, j, left, right, down, up, (count, 5 * q + j), *outer[axis])
            return carry

        lax.fori_loop(0, 5, weights, 0)
        launch(1, axis, count)

    for axis in (1, 0):

        def variable(v, carry):
            up, down = sends[1][2 * axis], sends[1][2 * axis + 1]
            low, high = masks[axis]
            step = spans if axis == 0 else 1

            def body(q, carry):
                for j in range(5):
                    pts = points(axis, q, j)
                    parts = fold([state[v, p] for p in pts])
                    left, right = traces(parts)
                    jump_left = jnp.where(low, 0.0, rolled(right, step, 0)) - left
                    jump_right = jnp.where(high, 0.0, rolled(left, -step, 0)) - right
                    if axis == 0:
                        jump_left = jnp.where(closed_low, 0.0, jump_left)
                        jump_right = jnp.where(closed_high, 0.0, jump_right)
                    gradient = slope(parts, jump_left, jump_right)
                    parts = fold([nu[p] * g for p, g in zip(pts, gradient)])
                    left, right = traces(parts)
                    store_pair(work, j, left, right, down, up, (v, 5 * q + j), *outer[axis])
                    before = jnp.where(low, 0.0, rolled(right, step, 0))
                    after = jnp.where(high, 0.0, rolled(left, -step, 0))
                    if axis == 0:
                        before = jnp.where(closed_low, -left, before)
                        after = jnp.where(closed_high, -right, after)
                    for p, value in zip(pts, slope(parts, before - left, after - right)):
                        if axis == 1:
                            acc[v, p] = value
                        else:
                            acc[v, p] += value
                return carry

            lax.fori_loop(0, 5, body, 0)
            launch(1, axis, v)
            return carry

        lax.fori_loop(0, count, variable, 0)

    lane = lax.broadcasted_iota(jnp.int32, (rows, lanes), 1)
    first, last = lane == 0, lane == lanes - 1

    def store(v):
        return pltpu.make_async_copy(acc.at[v], partial.at[v], store_sem.at[v])

    def normal(v, carry):
        def body(q, carry):
            for j in range(5):
                pts = points(2, q, j)
                parts = fold([state[v, p] for p in pts])
                left, right = traces(parts)
                jump_left = jnp.where(first, 0.0, rolled(right, 1, 1) - left)
                jump_right = jnp.where(last, 0.0, rolled(left, -1, 1) - right)
                gradient = slope(parts, jump_left, jump_right)
                parts = fold([nu[p] * g for p, g in zip(pts, gradient)])
                left, right = traces(parts)
                jump_left = jnp.where(first, -left, rolled(right, 1, 1)) - left
                jump_right = jnp.where(last, -right, rolled(left, -1, 1)) - right
                for p, value in zip(pts, slope(parts, jump_left, jump_right)):
                    acc[v, p] += value
            return carry

        lax.fori_loop(0, 5, body, 0)
        store(v).start()
        return carry

    lax.fori_loop(0, count, normal, 0)

    for v in range(count):
        store(v).wait()
    for dx, dy in offsets:
        guarded(reachable(dx), lambda dx=dx, dy=dy: eps_copy(dx, dy).wait_send())
    for stage in range(2):
        for k in range(4):
            for v in range(count + stage):
                guarded(reachable(ways[k][0]), lambda k=k, v=v: message(stage, k, v).wait_send())
                guarded(reachable(-ways[k][0]), lambda k=k, v=v: message(stage, k, v).wait_recv())


def ghost_kernel(chords, spans, *refs):
    partial, nu, faces_c, faces_s = refs[:4]
    ghosts, flux_ghosts, weights = refs[4:8], refs[8:12], refs[12:16]
    out, gain, edge, beta, outside, alpha = refs[16:]
    v = pl.program_id(0)
    rows, lanes = nu.shape[1:]
    row = lax.broadcasted_iota(jnp.int32, (rows, lanes), 0)
    place = lax.axis_index("chord")
    closed_low = row < jnp.where(place == 0, spans, 0)
    closed_high = row >= jnp.where(place == lax.axis_size("chord") - 1, rows - spans, rows)

    for axis, faces in ((0, faces_c), (1, faces_s)):
        up, down = ghosts[2 * axis], ghosts[2 * axis + 1]
        f_up, f_down = flux_ghosts[2 * axis], flux_ghosts[2 * axis + 1]
        b_up, b_down = weights[2 * axis], weights[2 * axis + 1]
        low, high = row_masks(axis, chords, spans, lanes)
        step = spans if axis == 0 else 1
        rows_low = outer_rows(axis, chords, spans, False)
        rows_high = outer_rows(axis, chords, spans, True)
        open_low, open_high = low, high
        if axis == 0:
            open_low = low & jnp.logical_not(closed_low)
            open_high = high & jnp.logical_not(closed_high)

        @pl.when(v == 0)
        def _():
            def body(q, carry):
                for j in range(5):
                    f = 5 * q + j
                    beta[axis, f, rows_low] = b_up[0, f]
                    beta[axis, f, rows_high] = b_down[0, f]
                    spread = []
                    for i, p in enumerate(points(axis, q, j)):
                        lift = jnp.where(high, float(HALF_RIGHT[i]), 0.0)
                        lift = jnp.where(low, float(HALF_LEFT[i]), lift)
                        spread.append(nu[p] * lift)
                    parts = fold(spread)
                    left, right = traces(parts)
                    edge[axis, 2 * f] = left
                    edge[axis, 2 * f + 1] = right
                    for i, value in enumerate(slope(parts, -left, -right)):
                        gain[axis, 5 * f + i] = value
                return carry

            lax.fori_loop(0, 5, body, 0)

        def gather(q, carry):
            for j in range(5):
                f = 5 * q + j
                outside[f, rows_low] = up[0, f]
                outside[f, rows_high] = down[0, f]
                alpha[f, rows_low] = f_up[0, f]
                alpha[f, rows_high] = f_down[0, f]
            return carry

        lax.fori_loop(0, 5, gather, 0)

        def body(q, carry):
            for j in range(5):
                f = 5 * q + j
                opened = open_low | open_high
                ghost = jnp.where(opened, outside[f], 0.0)
                flux = jnp.where(opened, alpha[f] + beta[axis, f] * faces[0, f], 0.0)
                before = jnp.where(low, flux, rolled(edge[axis, 2 * f + 1] * ghost, step, 0))
                after = jnp.where(high, flux, rolled(edge[axis, 2 * f] * ghost, -step, 0))
                h = [float(x) for x in HALF_LEFT]
                diff, both = before - after, before + after
                even = [0.5 * (h[i] + h[4 - i]) * diff for i in range(3)]
                odd = [0.5 * (h[i] - h[4 - i]) * both for i in range(2)]
                lifts = [even[0] + odd[0], even[1] + odd[1], even[2], even[1] - odd[1], even[0] - odd[0]]
                for i, p in enumerate(points(axis, q, j)):
                    value = gain[axis, 5 * f + i] * ghost + lifts[i]
                    if axis == 0:
                        out[0, p] = partial[0, p] + value
                    else:
                        out[0, p] += value
            return carry

        lax.fori_loop(0, 5, body, 0)


def shards(state):
    count, npts, chords, spans, lanes = state.shape
    rows = chords * spans
    flat = state.reshape(count, npts, rows, lanes)
    f32 = jnp.float32
    sizes = (lax.axis_size("chord"), lax.axis_size("span"))

    def message(n, k):
        return (n, 25, spans if k < 2 else chords, lanes)

    def full(*shape):
        return jax.ShapeDtypeStruct(shape, f32)

    vmem = pl.BlockSpec(memory_space=pltpu.VMEM)
    hbm = pl.BlockSpec(memory_space=pl.ANY)
    nu, faces_c, faces_s, partial, *moved = pl.pallas_call(
        functools.partial(local_kernel, sizes, count, chords, spans),
        in_specs=[hbm],
        out_specs=[vmem] * 3 + [hbm] * 9,
        out_shape=[full(npts, rows, lanes)] + [full(count, 25, rows, lanes)] * 2
        + [full(count, npts, rows, lanes)]
        + [full(*message(count, k)) for k in range(4)]
        + [full(*message(count + 1, k)) for k in range(4)],
        scratch_shapes=[
            pltpu.VMEM((count, npts, rows, lanes), f32),
            pltpu.VMEM((count, npts, rows, lanes), f32),
            pltpu.VMEM((3, 3, rows, lanes), f32),
            pltpu.VMEM((npts, rows, lanes), f32),
            pltpu.VMEM((rows, lanes), f32),
        ]
        + [pltpu.VMEM(message(count, k), f32) for k in range(4)]
        + [pltpu.VMEM(message(count + 1, k), f32) for k in range(4)]
        + [
            pltpu.SemaphoreType.DMA((count,)),
            pltpu.SemaphoreType.DMA((count,)),
            pltpu.SemaphoreType.DMA((9,)),
            pltpu.SemaphoreType.DMA((9,)),
            pltpu.SemaphoreType.DMA((2, 4, count + 1)),
            pltpu.SemaphoreType.DMA((2, 4, count + 1)),
        ],
        compiler_params=pltpu.CompilerParams(collective_id=0, has_side_effects=True),
    )(flat)

    def block(n, width, fixed=None):
        shape = (1, n, width, lanes)
        return pl.BlockSpec(shape, lambda v: (v if fixed is None else fixed, 0, 0, 0))

    widths = [spans, spans, chords, chords]
    per_variable = block(npts, rows)
    residual = pl.pallas_call(
        functools.partial(ghost_kernel, chords, spans),
        grid=(count,),
        in_specs=[
            per_variable,
            pl.BlockSpec((npts, rows, lanes), lambda v: (0, 0, 0)),
            block(25, rows),
            block(25, rows),
        ]
        + [block(25, w) for w in widths] * 2
        + [block(25, w, count) for w in widths],
        out_specs=per_variable,
        out_shape=full(*flat.shape),
        scratch_shapes=[
            pltpu.VMEM((2, npts, rows, lanes), f32),
            pltpu.VMEM((2, 50, rows, lanes), f32),
            pltpu.VMEM((2, 25, rows, lanes), f32),
            pltpu.VMEM((25, rows, lanes), f32),
            pltpu.VMEM((25, rows, lanes), f32),
        ],
    )(partial, nu, faces_c, faces_s, *moved, *moved[4:])
    return residual.reshape(state.shape), nu.reshape(npts, chords, spans, lanes)


def solution(mesh):
    in_specs = (P(None, None, "chord", "span", None),)
    out_specs = (P(None, None, "chord", "span", None), P(None, "chord", "span", None))
    return jax.shard_map(shards, mesh=mesh, in_specs=in_specs, out_specs=out_specs, check_vma=False)
```

time: 68.2 us -> 29.9 us (0.44)
  starting transfers between devices: 26 us -> 0 us
  waiting for transfers between devices: 9.85 us -> 0 us
  Pallas kernels: 24.9 us -> 28.2 us
  other arithmetic: 2.89 us -> 0 us
  local copies, waits for them, and re-layouts: 3.08 us -> 0.79 us
    ppermute x12 -> x0, starting transfers between devices: 26 us -> none  [along(): return lax.ppermute(block, axis, route)]
    ppermute x12 -> x0, waiting for transfers between devices: 9.85 us -> none  [along(): return lax.ppermute(block, axis, route)]
    pallas_call x3 -> x2, Pallas kernels: 24.9 us -> 28.2 us  [the longest x1 21.1 us: shards(): pl.pallas_call(functools.partial(local_kernel, sizes, count, chords, span...]
    unnamed x28 -> x3, local copies, waits for them, and re-layouts: 2.3 us -> 0.79 us
    concatenate x2 -> x0, other arithmetic: 1.48 us -> none  [grown(): eps = jnp.concatenate([before, eps, after], axis=dim)]
    unnamed x2 -> x0, other arithmetic: 1.4 us -> none
    slice x1 -> x0, local copies, waits for them, and re-layouts: 0.77 us -> none  [grown(): before = along(lax.slice_in_dim(eps, length - 1, length, axis=dim), axis, 1)]
  transfers between devices with their start and end apart: 12 -> 0, of which waited for: 4 -> 0; matrix products, arithmetic and copies ran while one was open for 4% -> 0% of each run, Pallas kernels for 10% -> 0%
where the time goes in v1:
time: 29.9 us; the launch traced here: 29.7 us
  Pallas kernels  28.2 us (94%)
  local copies, waits for them, and re-layouts  0.79 us (3%)
  between operations  0.66 us (2%)
    pallas_call x1, Pallas kernels, shards(): pl.pallas_call(functools.partial(local_kernel, sizes, count, chords, span...  21.1 us
    pallas_call x1, Pallas kernels, shards(): pl.pallas_call(functools.partial(ghost_kernel, chords, spans), grid=(coun...  7.11 us
    unnamed x3, local copies, waits for them, and re-layouts  0.79 us

profile of v1, /device:TPU:0, one launch (start us, length us, event | category | flops | bytes accessed | tf_op | source)
XLA Modules:
  0.0 29.7 jit_solution(8640192470029961147)
XLA Ops:
  0.6 21.1 %shard_map.30 = (f32[125,8,128]{2,1,0:T(8,128)}, f32[5,25,8,128]{3,2,1,0:T(8,128)}, f32[5,25,8,128]{3,2,1,0:T(8,128)}, f32[5,125,8,128]{3,2,1,0:T(8,128)}, f32[5...) custom-call(f32[5,125,8,128]{3,2,1,0:T(8,128)} %bitcast.4), custom_call_target="tpu_custom_call" | custom-call | tf_op jit(solution)/shard_map/pallas_call | solution.py:534
  21.8 0.0 copy-start
  21.8 7.1 %shard_map.31 = f32[5,125,8,128]{3,2,1,0:T(8,128)} custom-call(f32[5,125,8,128]{3,2,1,0:T(8,128)} %get-tuple-element.14.refs_0_, f32[125,8,128]{2,1,0:T(8,128)} %get-tuple-element.15.refs_1_, f32[5,25,8,128]{3,2,1,0:T(8,128)} %get-tuple-element.16.refs_2_, f32[5,25,8,128]{3,2,1,0:T(8,128)} %get-tuple-element.17.refs_3_, ...), custom_call_target="tpu_custom_call" | custom-call | tf_op jit(solution)/shard_map/pallas_call | solution.py:568
  28.9 0.0 copy-done
  28.9 0.8 %copy.4 = f32[125,4,2,128]{3,2,1,0:T(2,128)} copy(f32[125,4,2,128]{3,2,1,0:T(2,128)S(1)} %bitcast.5) | data formatting | bytes 1024000
Async XLA Ops:
  21.8 7.1 %copy-start = (f32[125,8,128]{2,1,0:T(8,128)S(1)}, f32[125,8,128]{2,1,0:T(8,128)}, u32[]{:S(2)}) copy-start(f32[125,8,128]{2,1,0:T(8,128)} %get-tuple-element.15.refs_1_) | copy-start | bytes 1536004

commit v2 on v1

--- a/solution.py
+++ b/solution.py
@@ -9,6 +9,7 @@
 from jax.experimental.pallas import tpu as pltpu
 from jax.sharding import PartitionSpec as P
 
+VMEM_BYTES = 24 * 2**20
 EPS_SCALE = 0.01
 SENSOR_CENTRE = -3.0
 SENSOR_WIDTH = 1.5
@@ -163,9 +164,19 @@
     return pltpu.roll(value, shift % size, axis)
 
 
+LOWER = [float((1.0 - x) / 2.0) for x in NODES]
+UPPER = [float((1.0 + x) / 2.0) for x in NODES]
+
+
+def along_lanes(line):
+    lanes = line.shape[1]
+    lane = lax.broadcasted_iota(jnp.int32, line.shape, 1)
+    before = jnp.where(lane == 0, 0.0, rolled(line, 1, 1))
+    after = jnp.where(lane == lanes - 1, 0.0, rolled(line, -1, 1))
+    return jnp.maximum(line, before), jnp.maximum(line, after)
+
+
 def interpolate(neighbours, nu):
-    rows, lanes = nu.shape[1:]
-    lane = lax.broadcasted_iota(jnp.int32, (rows, lanes), 1)
     corner = {}
     for x in range(2):
         for y in range(2):
@@ -173,12 +184,8 @@
                 jnp.maximum(neighbours[x][y], neighbours[x + 1][y]),
                 jnp.maximum(neighbours[x][y + 1], neighbours[x + 1][y + 1]),
             )
-            before = jnp.where(lane == 0, 0.0, rolled(line, 1, 1))
-            after = jnp.where(lane == lanes - 1, 0.0, rolled(line, -1, 1))
-            corner[x, y, 0] = jnp.maximum(line, before)
-            corner[x, y, 1] = jnp.maximum(line, after)
-    lower = [float((1.0 - x) / 2.0) for x in NODES]
-    upper = [float((1.0 + x) / 2.0) for x in NODES]
+            corner[x, y, 0], corner[x, y, 1] = along_lanes(line)
+    lower, upper = LOWER, UPPER
     for a in range(5):
         face = {
             (y, z): lower[a] * corner[0, y, z] + upper[a] * corner[1, y, z]
@@ -189,6 +196,7 @@
             edge = [lower[b] * face[0, z] + upper[b] * face[1, z] for z in range(2)]
             for c in range(5):
                 nu[25 * a + 5 * b + c] = lower[c] * edge[0] + upper[c] * edge[1]
+    return corner
 
 
 def row_masks(axis, chords, spans, lanes):
@@ -214,14 +222,13 @@
 
 def local_kernel(sizes, count, chords, spans, *refs):
     state_hbm = refs[0]
-    nu, faces_c, faces_s, partial = refs[1:5]
-    ghosts = refs[5:9]
-    flux_ghosts = refs[9:13]
+    nu, result = refs[1:3]
     (
-        state, acc, around, work, eps_out,
+        state, acc, around, work, eps_out, faces_c, faces_s, gain, edge, beta, outside, alpha,
         t0, t1, t2, t3, f0, f1, f2, f3,
-        load_sem, store_sem, eps_send, eps_recv, send_sem, recv_sem,
-    ) = refs[13:]
+    ) = refs[3:23]
+    ghosts, flux_ghosts = refs[23:27], refs[27:31]
+    load_sem, store_sem, eps_send, eps_recv, send_sem, recv_sem = refs[31:]
     sends = ((t0, t1, t2, t3), (f0, f1, f2, f3))
     lands = (ghosts, flux_ghosts)
     rows, lanes = nu.shape[1:]
@@ -257,13 +264,6 @@
             pl.semaphore_signal(barrier, inc=1, device_id=partner(dx, dy), device_id_type=mesh_id)
 
         guarded(reachable(dx), greet)
-
-    load(0).wait()
-    eps = sensor(lambda p: state[0, p], work)
-    eps_out[...] = eps
-    around[1, 1] = eps
-    sides = jnp.where(me_c > 0, 1, 0) + jnp.where(me_c + 1 < chord_size, 1, 0)
-    pl.semaphore_wait(barrier, 2 + 3 * sides)
 
     def eps_copy(dx, dy):
         slot = 3 * (dx + 1) + dy + 1
@@ -273,9 +273,6 @@
             device_id=partner(dx, dy), device_id_type=mesh_id,
         )
 
-    for dx, dy in offsets:
-        guarded(reachable(dx), lambda dx=dx, dy=dy: eps_copy(dx, dy).start())
-
     ways = ((1, 0), (-1, 0), (0, 1), (0, -1))
 
     def message(stage, k, v):
@@ -293,27 +290,41 @@
     masks = [row_masks(axis, chords, spans, lanes) for axis in range(2)]
     outer = [[outer_rows(axis, chords, spans, last) for last in (False, True)] for axis in range(2)]
 
-    def send_traces(v, carry):
-        @pl.when(v > 0)
-        def _():
-            load(v).wait()
-
+    def send_traces(axis, v):
+        up, down = sends[0][2 * axis], sends[0][2 * axis + 1]
+        faces = (faces_c, faces_s)[axis]
+
+        def body(q, carry):
+            for j in range(5):
+                left, right = traces(fold([state[v, p] for p in points(axis, q, j)]))
+                faces[v, 5 * q + j] = jnp.where(masks[axis][0], left, right)
+                store_pair(work, j, left, right, down, up, (v, 5 * q + j), *outer[axis])
+            return carry
+
+        lax.fori_loop(0, 5, body, 0)
+
+    load(0).wait()
+    send_traces(1, 0)
+    sides = jnp.where(me_c > 0, 1, 0) + jnp.where(me_c + 1 < chord_size, 1, 0)
+    pl.semaphore_wait(barrier, 2 + 3 * sides)
+    launch(0, 1, 0)
+    eps = sensor(lambda p: state[0, p], work)
+    eps_out[...] = eps
+    around[1, 1] = eps
+    for dx, dy in offsets:
+        guarded(reachable(dx), lambda dx=dx, dy=dy: eps_copy(dx, dy).start())
+
+    send_traces(0, 0)
+    launch(0, 0, 0)
+
+    def later_traces(v, carry):
+        load(v).wait()
         for axis in (1, 0):
-            up, down = sends[0][2 * axis], sends[0][2 * axis + 1]
-            faces = (faces_c, faces_s)[axis]
-
-            def body(q, carry):
-                for j in range(5):
-                    left, right = traces(fold([state[v, p] for p in points(axis, q, j)]))
-                    faces[v, 5 * q + j] = jnp.where(masks[axis][0], left, right)
-                    store_pair(work, j, left, right, down, up, (v, 5 * q + j), *outer[axis])
-                return carry
-
-            lax.fori_loop(0, 5, body, 0)
+            send_traces(axis, v)
             launch(0, axis, v)
         return carry
 
-    lax.fori_loop(0, count, send_traces, 0)
+    lax.fori_loop(1, count, later_traces, 0)
 
     row = lax.broadcasted_iota(jnp.int32, (rows, lanes), 0)
     for dx, dy in offsets:
@@ -321,40 +332,57 @@
 
     have_low = jnp.where(me_c > 0, spans, 0)
     have_high = jnp.where(me_c + 1 < chord_size, rows, rows - spans)
+    low_s, high_s = masks[1]
+    low_c, high_c = masks[0]
     column = []
     for x in range(3):
         mine, left, right = around[x, 1], around[x, 0], around[x, 2]
         column.append([
-            jnp.where(masks[1][0], rolled(left, 1 - spans, 0), rolled(mine, 1, 0)),
+            jnp.where(low_s, rolled(left, 1 - spans, 0), rolled(mine, 1, 0)),
             mine,
-            jnp.where(masks[1][1], rolled(right, spans - 1, 0), rolled(mine, -1, 0)),
+            jnp.where(high_s, rolled(right, spans - 1, 0), rolled(mine, -1, 0)),
+            jnp.where(low_s, rolled(left, 2 - spans, 0), rolled(right, spans - 2, 0)),
         ])
-    neighbours = [[], [], []]
-    for y in range(3):
-        inner = column[1][y]
-        below = jnp.where(masks[0][0], rolled(column[0][y], spans, 0), rolled(inner, spans, 0))
-        above = jnp.where(masks[0][1], rolled(column[2][y], -spans, 0), rolled(inner, -spans, 0))
-        neighbours[0].append(jnp.where(row < spans - have_low, 0.0, below))
-        neighbours[1].append(inner)
-        neighbours[2].append(jnp.where(row >= have_high, 0.0, above))
-    interpolate(neighbours, nu)
-
     closed_low = row < spans - have_low
     closed_high = row >= have_high
-
-    for axis in (1, 0):
-        up, down = sends[1][2 * axis], sends[1][2 * axis + 1]
-
-        def weights(q, carry):
-            for j in range(5):
-                local = [nu[p] for p in points(axis, q, j)]
-                left = sum(float(LEFT[i] * HALF_LEFT[i]) * local[i] for i in range(5))
-                right = sum(float(RIGHT[i] * HALF_RIGHT[i]) * local[i] for i in range(5))
-                store_pair(work, j, left, right, down, up, (count, 5 * q + j), *outer[axis])
-            return carry
-
-        lax.fori_loop(0, 5, weights, 0)
-        launch(1, axis, count)
+    neighbours = [[], [], [], []]
+    for y in range(4):
+        inner = column[1][y]
+        below = jnp.where(low_c, rolled(column[0][y], spans, 0), rolled(inner, spans, 0))
+        above = jnp.where(high_c, rolled(column[2][y], -spans, 0), rolled(inner, -spans, 0))
+        beyond = jnp.where(
+            low_c, rolled(column[0][y], 2 * spans, 0), rolled(column[2][y], -2 * spans, 0)
+        )
+        neighbours[0].append(jnp.where(closed_low, 0.0, below))
+        neighbours[1].append(inner)
+        neighbours[2].append(jnp.where(closed_high, 0.0, above))
+        neighbours[3].append(beyond)
+    corner = interpolate(neighbours, nu)
+    near_weight = sum(float(LEFT[i] * HALF_LEFT[i] * (1.0 - NODES[i]) / 2.0) for i in range(5))
+    far_weight = sum(float(LEFT[i] * HALF_LEFT[i] * (1.0 + NODES[i]) / 2.0) for i in range(5))
+    for axis in range(2):
+        low = masks[axis][0]
+        sign = jnp.where(low, -1.0, 1.0)
+        weight = {}
+        for t in range(2):
+            pair = []
+            for o in (t, t + 1):
+                if axis == 0:
+                    pair += [jnp.where(low, neighbours[0][o], neighbours[2][o]), neighbours[3][o]]
+                else:
+                    pair += [jnp.where(low, neighbours[o][0], neighbours[o][2]), neighbours[o][3]]
+            line = jnp.maximum(jnp.maximum(pair[0], pair[1]), jnp.maximum(pair[2], pair[3]))
+            far = along_lanes(line)
+            for z in range(2):
+                if axis == 0:
+                    near = jnp.where(low, corner[0, t, z], corner[1, t, z])
+                else:
+                    near = jnp.where(low, corner[t, 0, z], corner[t, 1, z])
+                weight[t, z] = sign * (near_weight * near + far_weight * far[z])
+        for m in range(5):
+            ends = [LOWER[m] * weight[0, z] + UPPER[m] * weight[1, z] for z in range(2)]
+            for c in range(5):
+                beta[axis, 5 * m + c] = LOWER[c] * ends[0] + UPPER[c] * ends[1]
 
     for axis in (1, 0):
 
@@ -399,7 +427,27 @@
     first, last = lane == 0, lane == lanes - 1
 
     def store(v):
-        return pltpu.make_async_copy(acc.at[v], partial.at[v], store_sem.at[v])
+        return pltpu.make_async_copy(acc.at[v], result.at[v], store_sem.at[v])
+
+    for axis in range(2):
+        low, high = masks[axis]
+
+        def gains(q, carry):
+            for j in range(5):
+                f = 5 * q + j
+                spread = []
+                for i, p in enumerate(points(axis, q, j)):
+                    lift = jnp.where(high, float(HALF_RIGHT[i]), 0.0)
+                    spread.append(nu[p] * jnp.where(low, float(HALF_LEFT[i]), lift))
+                parts = fold(spread)
+                left, right = traces(parts)
+                edge[axis, 2 * f] = left
+                edge[axis, 2 * f + 1] = right
+                for i, value in enumerate(slope(parts, -left, -right)):
+                    gain[axis, 5 * f + i] = value
+            return carry
+
+        lax.fori_loop(0, 5, gains, 0)
 
     def normal(v, carry):
         def body(q, carry):
@@ -419,10 +467,68 @@
             return carry
 
         lax.fori_loop(0, 5, body, 0)
-        store(v).start()
         return carry
 
     lax.fori_loop(0, count, normal, 0)
+
+    def arrived(axis, v):
+        for k in (2 * axis, 2 * axis + 1):
+            for stage in range(2):
+                guarded(
+                    reachable(-ways[k][0]),
+                    lambda k=k, stage=stage: message(stage, k, v).wait_recv(),
+                )
+
+    for axis in (0, 1):
+
+        def correct(v, carry):
+            arrived(axis, v)
+            up, down = ghosts[2 * axis], ghosts[2 * axis + 1]
+            f_up, f_down = flux_ghosts[2 * axis], flux_ghosts[2 * axis + 1]
+            faces = (faces_c, faces_s)[axis]
+            low, high = masks[axis]
+            rows_low, rows_high = outer[axis]
+            step = spans if axis == 0 else 1
+            opened = low | high
+            if axis == 0:
+                opened = opened & jnp.logical_not(closed_low | closed_high)
+
+            def gather(q, carry):
+                for j in range(5):
+                    f = 5 * q + j
+                    outside[f, rows_low] = up[v, f]
+                    outside[f, rows_high] = down[v, f]
+                    alpha[f, rows_low] = f_up[v, f]
+                    alpha[f, rows_high] = f_down[v, f]
+                return carry
+
+            lax.fori_loop(0, 5, gather, 0)
+
+            def body(q, carry):
+                for j in range(5):
+                    f = 5 * q + j
+                    ghost = jnp.where(opened, outside[f], 0.0)
+                    flux = jnp.where(opened, alpha[f] + beta[axis, f] * faces[v, f], 0.0)
+                    before = jnp.where(low, flux, rolled(edge[axis, 2 * f + 1] * ghost, step, 0))
+                    after = jnp.where(high, flux, rolled(edge[axis, 2 * f] * ghost, -step, 0))
+                    h = [float(x) for x in HALF_LEFT]
+                    diff, both = before - after, before + after
+                    even = [0.5 * (h[i] + h[4 - i]) * diff for i in range(3)]
+                    odd = [0.5 * (h[i] - h[4 - i]) * both for i in range(2)]
+                    lifts = [
+                        even[0] + odd[0], even[1] + odd[1], even[2],
+                        even[1] - odd[1], even[0] - odd[0],
+                    ]
+                    for i, p in enumerate(points(axis, q, j)):
+                        acc[v, p] += gain[axis, 5 * f + i] * ghost + lifts[i]
+                return carry
+
+            lax.fori_loop(0, 5, body, 0)
+            if axis == 1:
+                store(v).start()
+            return carry
+
+        lax.fori_loop(0, count, correct, 0)
 
     for v in range(count):
         store(v).wait()
@@ -430,90 +536,11 @@
         guarded(reachable(dx), lambda dx=dx, dy=dy: eps_copy(dx, dy).wait_send())
     for stage in range(2):
         for k in range(4):
-            for v in range(count + stage):
-                guarded(reachable(ways[k][0]), lambda k=k, v=v: message(stage, k, v).wait_send())
-                guarded(reachable(-ways[k][0]), lambda k=k, v=v: message(stage, k, v).wait_recv())
-
-
-def ghost_kernel(chords, spans, *refs):
-    partial, nu, faces_c, faces_s = refs[:4]
-    ghosts, flux_ghosts, weights = refs[4:8], refs[8:12], refs[12:16]
-    out, gain, edge, beta, outside, alpha = refs[16:]
-    v = pl.program_id(0)
-    rows, lanes = nu.shape[1:]
-    row = lax.broadcasted_iota(jnp.int32, (rows, lanes), 0)
-    place = lax.axis_index("chord")
-    closed_low = row < jnp.where(place == 0, spans, 0)
-    closed_high = row >= jnp.where(place == lax.axis_size("chord") - 1, rows - spans, rows)
-
-    for axis, faces in ((0, faces_c), (1, faces_s)):
-        up, down = ghosts[2 * axis], ghosts[2 * axis + 1]
-        f_up, f_down = flux_ghosts[2 * axis], flux_ghosts[2 * axis + 1]
-        b_up, b_down = weights[2 * axis], weights[2 * axis + 1]
-        low, high = row_masks(axis, chords, spans, lanes)
-        step = spans if axis == 0 else 1
-        rows_low = outer_rows(axis, chords, spans, False)
-        rows_high = outer_rows(axis, chords, spans, True)
-        open_low, open_high = low, high
-        if axis == 0:
-            open_low = low & jnp.logical_not(closed_low)
-            open_high = high & jnp.logical_not(closed_high)
-
-        @pl.when(v == 0)
-        def _():
-            def body(q, carry):
-                for j in range(5):
-                    f = 5 * q + j
-                    beta[axis, f, rows_low] = b_up[0, f]
-                    beta[axis, f, rows_high] = b_down[0, f]
-                    spread = []
-                    for i, p in enumerate(points(axis, q, j)):
-                        lift = jnp.where(high, float(HALF_RIGHT[i]), 0.0)
-                        lift = jnp.where(low, float(HALF_LEFT[i]), lift)
-                        spread.append(nu[p] * lift)
-                    parts = fold(spread)
-                    left, right = traces(parts)
-                    edge[axis, 2 * f] = left
-                    edge[axis, 2 * f + 1] = right
-                    for i, value in enumerate(slope(parts, -left, -right)):
-                        gain[axis, 5 * f + i] = value
-                return carry
-
-            lax.fori_loop(0, 5, body, 0)
-
-        def gather(q, carry):
-            for j in range(5):
-                f = 5 * q + j
-                outside[f, rows_low] = up[0, f]
-                outside[f, rows_high] = down[0, f]
-                alpha[f, rows_low] = f_up[0, f]
-                alpha[f, rows_high] = f_down[0, f]
-            return carry
-
-        lax.fori_loop(0, 5, gather, 0)
-
-        def body(q, carry):
-            for j in range(5):
-                f = 5 * q + j
-                opened = open_low | open_high
-                ghost = jnp.where(opened, outside[f], 0.0)
-                flux = jnp.where(opened, alpha[f] + beta[axis, f] * faces[0, f], 0.0)
-                before = jnp.where(low, flux, rolled(edge[axis, 2 * f + 1] * ghost, step, 0))
-                after = jnp.where(high, flux, rolled(edge[axis, 2 * f] * ghost, -step, 0))
-                h = [float(x) for x in HALF_LEFT]
-                diff, both = before - after, before + after
-                even = [0.5 * (h[i] + h[4 - i]) * diff for i in range(3)]
-                odd = [0.5 * (h[i] - h[4 - i]) * both for i in range(2)]
-                lifts = [even[0] + odd[0], even[1] + odd[1], even[2], even[1] - odd[1], even[0] - odd[0]]
-                for i, p in enumerate(points(axis, q, j)):
-                    value = gain[axis, 5 * f + i] * ghost + lifts[i]
-                    if axis == 0:
-                        out[0, p] = partial[0, p] + value
-                    else:
-                        out[0, p] += value
-            return carry
-
-        lax.fori_loop(0, 5, body, 0)
+            for v in range(count):
+                guarded(
+                    reachable(ways[k][0]),
+                    lambda stage=stage, k=k, v=v: message(stage, k, v).wait_send(),
+                )
 
 
 def shards(state):
@@ -531,61 +558,41 @@
 
     vmem = pl.BlockSpec(memory_space=pltpu.VMEM)
     hbm = pl.BlockSpec(memory_space=pl.ANY)
-    nu, faces_c, faces_s, partial, *moved = pl.pallas_call(
+    nu, residual = pl.pallas_call(
         functools.partial(local_kernel, sizes, count, chords, spans),
-        in_specs=[hbm],
-        out_specs=[vmem] * 3 + [hbm] * 9,
-        out_shape=[full(npts, rows, lanes)] + [full(count, 25, rows, lanes)] * 2
-        + [full(count, npts, rows, lanes)]
-        + [full(*message(count, k)) for k in range(4)]
-        + [full(*message(count + 1, k)) for k in range(4)],
+        in_specs=[pl.BlockSpec(memory_space=pltpu.HBM)],
+        out_specs=[vmem, hbm],
+        out_shape=[full(npts, rows, lanes), full(count, npts, rows, lanes)],
         scratch_shapes=[
-            pltpu.VMEM((count, npts, rows, lanes), f32),
-            pltpu.VMEM((count, npts, rows, lanes), f32),
-            pltpu.VMEM((3, 3, rows, lanes), f32),
-            pltpu.VMEM((npts, rows, lanes), f32),
-            pltpu.VMEM((rows, lanes), f32),
+            pltpu.VMEM(shape, f32)
+            for shape in [
+                (count, npts, rows, lanes),
+                (count, npts, rows, lanes),
+                (3, 3, rows, lanes),
+                (npts, rows, lanes),
+                (rows, lanes),
+                (count, 25, rows, lanes),
+                (count, 25, rows, lanes),
+                (2, npts, rows, lanes),
+                (2, 50, rows, lanes),
+                (2, 25, rows, lanes),
+                (25, rows, lanes),
+                (25, rows, lanes),
+            ]
+            + [message(count, k) for k in range(4)] * 4
         ]
-        + [pltpu.VMEM(message(count, k), f32) for k in range(4)]
-        + [pltpu.VMEM(message(count + 1, k), f32) for k in range(4)]
         + [
             pltpu.SemaphoreType.DMA((count,)),
             pltpu.SemaphoreType.DMA((count,)),
             pltpu.SemaphoreType.DMA((9,)),
             pltpu.SemaphoreType.DMA((9,)),
-            pltpu.SemaphoreType.DMA((2, 4, count + 1)),
-            pltpu.SemaphoreType.DMA((2, 4, count + 1)),
+            pltpu.SemaphoreType.DMA((2, 4, count)),
+            pltpu.SemaphoreType.DMA((2, 4, count)),
         ],
-        compiler_params=pltpu.CompilerParams(collective_id=0, has_side_effects=True),
+        compiler_params=pltpu.CompilerParams(
+            collective_id=0, has_side_effects=True, vmem_limit_bytes=VMEM_BYTES
+        ),
     )(flat)
-
-    def block(n, width, fixed=None):
-        shape = (1, n, width, lanes)
-        return pl.BlockSpec(shape, lambda v: (v if fixed is None else fixed, 0, 0, 0))
-
-    widths = [spans, spans, chords, chords]
-    per_variable = block(npts, rows)
-    residual = pl.pallas_call(
-        functools.partial(ghost_kernel, chords, spans),
-        grid=(count,),
-        in_specs=[
-            per_variable,
-            pl.BlockSpec((npts, rows, lanes), lambda v: (0, 0, 0)),
-            block(25, rows),
-            block(25, rows),
-        ]
-        + [block(25, w) for w in widths] * 2
-        + [block(25, w, count) for w in widths],
-        out_specs=per_variable,
-        out_shape=full(*flat.shape),
-        scratch_shapes=[
-            pltpu.VMEM((2, npts, rows, lanes), f32),
-            pltpu.VMEM((2, 50, rows, lanes), f32),
-            pltpu.VMEM((2, 25, rows, lanes), f32),
-            pltpu.VMEM((25, rows, lanes), f32),
-            pltpu.VMEM((25, rows, lanes), f32),
-        ],
-    )(partial, nu, faces_c, faces_s, *moved, *moved[4:])
     return residual.reshape(state.shape), nu.reshape(npts, chords, spans, lanes)
 
 

time: 29.9 us -> 30.1 us (level)
  local copies, waits for them, and re-layouts: 0.79 us -> 3.97 us
  Pallas kernels: 28.2 us -> 25.4 us
    pallas_call x1 -> x0, Pallas kernels: 7.11 us -> none  [shards(): pl.pallas_call(functools.partial(ghost_kernel, chords, spans), grid=(coun...]
    pallas_call x1, Pallas kernels: 21.1 us -> 25.4 us  [shards(): pl.pallas_call(functools.partial(local_kernel, sizes, count, chords, span...]
    unnamed x3 -> x4, local copies, waits for them, and re-layouts: 0.79 us -> 3.97 us
where the time goes in v2:
time: 30.1 us; the launch traced here: 30 us
  Pallas kernels  25.4 us (84%)
  local copies, waits for them, and re-layouts  3.97 us (13%)
  between operations  0.65 us (2%)
    pallas_call x1, Pallas kernels, shards(): pl.pallas_call(functools.partial(local_kernel, sizes, count, chords, span...  25.4 us
    unnamed x4, local copies, waits for them, and re-layouts  3.97 us

profile of v2, /device:TPU:0, one launch (start us, length us, event | category | flops | bytes accessed | tf_op | source)
XLA Modules:
  0.0 30.0 jit_solution(7792110567210705463)
XLA Ops:
  0.6 0.0 copy-start
  0.6 1.7 %copy-done = f32[5,125,4,2,128]{4,3,2,1,0:T(2,128)S(1)} copy-done((f32[5,125,4,2,128]{4,3,2,1,0:T(2,128)S(1)}, f32[5,125,4,2,128]{4,3,2,1,0:T(2,128)}, u32[]{:S(2)}) %copy-start) | copy-done | bytes 2560024
  2.4 25.4 %shard_map.30 = (f32[125,8,128]{2,1,0:T(8,128)S(1)}, f32[5,125,8,128]{3,2,1,0:T(8,128)S(1)}) custom-call(f32[5,125,8,128]{3,2,1,0:T(8,128)S(1)} %bitcast.3), custom_call_target="tpu_custom_call" | custom-call | tf_op jit(solution)/shard_map/pallas_call | solution.py:561
  27.7 1.5 %copy.5 = f32[5,125,4,2,128]{4,3,2,1,0:T(2,128)} copy(f32[5,125,4,2,128]{4,3,2,1,0:T(2,128)S(1)} %bitcast.4) | data formatting | bytes 5120000
  29.2 0.8 %copy.6 = f32[125,4,2,128]{3,2,1,0:T(2,128)} copy(f32[125,4,2,128]{3,2,1,0:T(2,128)S(1)} %bitcast.5) | data formatting | bytes 1024000
Async XLA Ops:
  0.6 1.7 %copy-start = (f32[5,125,4,2,128]{4,3,2,1,0:T(2,128)S(1)}, f32[5,125,4,2,128]{4,3,2,1,0:T(2,128)}, u32[]{:S(2)}) copy-start(f32[5,125,4,2,128]{4,3,2,1,0:T(2,128)} %param.1) | copy-start | bytes 7680004

commit v3 on v2

--- a/solution.py
+++ b/solution.py
@@ -221,26 +221,20 @@
 
 
 def local_kernel(sizes, count, chords, spans, *refs):
-    state_hbm = refs[0]
-    nu, result = refs[1:3]
+    state = refs[0]
+    nu, acc = refs[1:3]
     (
-        state, acc, around, work, eps_out, faces_c, faces_s, gain, edge, beta, outside, alpha,
+        around, work, eps_out, faces_c, faces_s, gain, edge, beta, outside, alpha,
         t0, t1, t2, t3, f0, f1, f2, f3,
-    ) = refs[3:23]
-    ghosts, flux_ghosts = refs[23:27], refs[27:31]
-    load_sem, store_sem, eps_send, eps_recv, send_sem, recv_sem = refs[31:]
+    ) = refs[3:21]
+    ghosts, flux_ghosts = refs[21:25], refs[25:29]
+    eps_send, eps_recv, send_sem, recv_sem = refs[29:]
     sends = ((t0, t1, t2, t3), (f0, f1, f2, f3))
     lands = (ghosts, flux_ghosts)
     rows, lanes = nu.shape[1:]
     chord_size, span_size = sizes
     me_c, me_s = lax.axis_index("chord"), lax.axis_index("span")
     mesh_id = pl.DeviceIdType.MESH
-
-    def load(v):
-        return pltpu.make_async_copy(state_hbm.at[v], state.at[v], load_sem.at[v])
-
-    for v in range(count):
-        load(v).start()
 
     def reachable(dx):
         if dx == 0:
@@ -303,7 +297,6 @@
 
         lax.fori_loop(0, 5, body, 0)
 
-    load(0).wait()
     send_traces(1, 0)
     sides = jnp.where(me_c > 0, 1, 0) + jnp.where(me_c + 1 < chord_size, 1, 0)
     pl.semaphore_wait(barrier, 2 + 3 * sides)
@@ -318,7 +311,6 @@
     launch(0, 0, 0)
 
     def later_traces(v, carry):
-        load(v).wait()
         for axis in (1, 0):
             send_traces(axis, v)
             launch(0, axis, v)
@@ -426,9 +418,6 @@
     lane = lax.broadcasted_iota(jnp.int32, (rows, lanes), 1)
     first, last = lane == 0, lane == lanes - 1
 
-    def store(v):
-        return pltpu.make_async_copy(acc.at[v], result.at[v], store_sem.at[v])
-
     for axis in range(2):
         low, high = masks[axis]
 
@@ -524,14 +513,10 @@
                 return carry
 
             lax.fori_loop(0, 5, body, 0)
-            if axis == 1:
-                store(v).start()
             return carry
 
         lax.fori_loop(0, count, correct, 0)
 
-    for v in range(count):
-        store(v).wait()
     for dx, dy in offsets:
         guarded(reachable(dx), lambda dx=dx, dy=dy: eps_copy(dx, dy).wait_send())
     for stage in range(2):
@@ -557,17 +542,14 @@
         return jax.ShapeDtypeStruct(shape, f32)
 
     vmem = pl.BlockSpec(memory_space=pltpu.VMEM)
-    hbm = pl.BlockSpec(memory_space=pl.ANY)
     nu, residual = pl.pallas_call(
         functools.partial(local_kernel, sizes, count, chords, spans),
-        in_specs=[pl.BlockSpec(memory_space=pltpu.HBM)],
-        out_specs=[vmem, hbm],
+        in_specs=[vmem],
+        out_specs=[vmem, vmem],
         out_shape=[full(npts, rows, lanes), full(count, npts, rows, lanes)],
         scratch_shapes=[
             pltpu.VMEM(shape, f32)
             for shape in [
-                (count, npts, rows, lanes),
-                (count, npts, rows, lanes),
                 (3, 3, rows, lanes),
                 (npts, rows, lanes),
                 (rows, lanes),
@@ -582,8 +564,6 @@
             + [message(count, k) for k in range(4)] * 4
         ]
         + [
-            pltpu.SemaphoreType.DMA((count,)),
-            pltpu.SemaphoreType.DMA((count,)),
             pltpu.SemaphoreType.DMA((9,)),
             pltpu.SemaphoreType.DMA((9,)),
             pltpu.SemaphoreType.DMA((2, 4, count)),

time: 30.1 us -> 26.6 us (0.88)
  Pallas kernels: 25.4 us -> 21.9 us
    pallas_call x1, Pallas kernels: 25.4 us -> 21.9 us  [shards(): pl.pallas_call(functools.partial(local_kernel, sizes, count, chords, span...]
where the time goes in v3:
time: 26.6 us; the launch traced here: 26.5 us
  Pallas kernels  21.9 us (82%)
  local copies, waits for them, and re-layouts  3.97 us (15%)
  between operations  0.65 us (2%)
    pallas_call x1, Pallas kernels, shards(): pl.pallas_call(functools.partial(local_kernel, sizes, count, chords, span...  21.9 us
    unnamed x4, local copies, waits for them, and re-layouts  3.97 us

profile of v3, /device:TPU:0, one launch (start us, length us, event | category | flops | bytes accessed | tf_op | source)
XLA Modules:
  0.0 26.5 jit_solution(9896368580162556822)
XLA Ops:
  0.6 0.0 copy-start
  0.6 1.7 %copy-done = f32[5,125,4,2,128]{4,3,2,1,0:T(2,128)S(1)} copy-done((f32[5,125,4,2,128]{4,3,2,1,0:T(2,128)S(1)}, f32[5,125,4,2,128]{4,3,2,1,0:T(2,128)}, u32[]{:S(2)}) %copy-start) | copy-done | bytes 2560024
  2.4 21.9 %shard_map.30 = (f32[125,8,128]{2,1,0:T(8,128)S(1)}, f32[5,125,8,128]{3,2,1,0:T(8,128)S(1)}) custom-call(f32[5,125,8,128]{3,2,1,0:T(8,128)S(1)} %bitcast.3), custom_call_target="tpu_custom_call" | custom-call | tf_op jit(solution)/shard_map/pallas_call | solution.py:545
  24.2 1.5 %copy.5 = f32[5,125,4,2,128]{4,3,2,1,0:T(2,128)} copy(f32[5,125,4,2,128]{4,3,2,1,0:T(2,128)S(1)} %bitcast.4) | data formatting | bytes 5120000
  25.7 0.8 %copy.6 = f32[125,4,2,128]{3,2,1,0:T(2,128)} copy(f32[125,4,2,128]{3,2,1,0:T(2,128)S(1)} %bitcast.5) | data formatting | bytes 1024000
Async XLA Ops:
  0.6 1.7 %copy-start = (f32[5,125,4,2,128]{4,3,2,1,0:T(2,128)S(1)}, f32[5,125,4,2,128]{4,3,2,1,0:T(2,128)}, u32[]{:S(2)}) copy-start(f32[5,125,4,2,128]{4,3,2,1,0:T(2,128)} %param.1) | copy-start | bytes 7680004

commit v4 on v2

--- a/solution.py
+++ b/solution.py
@@ -9,7 +9,7 @@
 from jax.experimental.pallas import tpu as pltpu
 from jax.sharding import PartitionSpec as P
 
-VMEM_BYTES = 24 * 2**20
+VMEM_BYTES = 52_500_000
 EPS_SCALE = 0.01
 SENSOR_CENTRE = -3.0
 SENSOR_WIDTH = 1.5
@@ -84,25 +84,28 @@
     return even - odd, even + odd
 
 
-def slope(parts, jump_left, jump_right):
+def slope(parts, before, after):
     s0, s1, mid, d0, d1 = parts
     h = [float(x) for x in HALF_LEFT]
-    diff = jump_left - jump_right
-    both = jump_left + jump_right
+    r = [float(x) for x in RIGHT]
+    if before is not None:
+        diff, both = before - after, before + after
     even, odd = [], []
     for i in range(3):
-        even.append(
-            float(0.5 * (DERIV[i, 0] - DERIV[i, 4])) * d0
-            + float(0.5 * (DERIV[i, 1] - DERIV[i, 3])) * d1
-            + 0.5 * (h[i] + h[4 - i]) * diff
+        lift = 0.5 * (h[i] + h[4 - i])
+        value = (
+            float(0.5 * (DERIV[i, 0] - DERIV[i, 4]) + lift * (r[0] - r[4])) * d0
+            + float(0.5 * (DERIV[i, 1] - DERIV[i, 3]) + lift * (r[1] - r[3])) * d1
         )
+        even.append(value if before is None else value + lift * diff)
     for i in range(2):
-        odd.append(
-            float(0.5 * (DERIV[i, 0] + DERIV[i, 4])) * s0
-            + float(0.5 * (DERIV[i, 1] + DERIV[i, 3])) * s1
-            + float(DERIV[i, 2]) * mid
-            + 0.5 * (h[i] - h[4 - i]) * both
+        lift = 0.5 * (h[i] - h[4 - i])
+        value = (
+            float(0.5 * (DERIV[i, 0] + DERIV[i, 4]) - lift * (r[0] + r[4])) * s0
+            + float(0.5 * (DERIV[i, 1] + DERIV[i, 3]) - lift * (r[1] + r[3])) * s1
+            + float(DERIV[i, 2] - 2.0 * lift * r[2]) * mid
         )
+        odd.append(value if before is None else value + lift * both)
     return [even[0] + odd[0], even[1] + odd[1], even[2], even[1] - odd[1], even[0] - odd[0]]
 
 
@@ -222,13 +225,13 @@
 
 def local_kernel(sizes, count, chords, spans, *refs):
     state_hbm = refs[0]
-    nu, result = refs[1:3]
+    nu, acc = refs[1:3]
     (
-        state, acc, around, work, eps_out, faces_c, faces_s, gain, edge, beta, outside, alpha,
+        state, grad, around, work, eps_out, faces_c, faces_s, gain, edge, beta, outside, alpha,
         t0, t1, t2, t3, f0, f1, f2, f3,
     ) = refs[3:23]
     ghosts, flux_ghosts = refs[23:27], refs[27:31]
-    load_sem, store_sem, eps_send, eps_recv, send_sem, recv_sem = refs[31:]
+    load_sem, eps_send, eps_recv, send_sem, recv_sem = refs[31:]
     sends = ((t0, t1, t2, t3), (f0, f1, f2, f3))
     lands = (ghosts, flux_ghosts)
     rows, lanes = nu.shape[1:]
@@ -325,6 +328,26 @@
         return carry
 
     lax.fori_loop(1, count, later_traces, 0)
+
+    lane = lax.broadcasted_iota(jnp.int32, (rows, lanes), 1)
+    first, last = lane == 0, lane == lanes - 1
+
+    def normal_gradient(v, carry):
+        def body(q, carry):
+            for j in range(5):
+                pts = points(2, q, j)
+                parts = fold([state[v, p] for p in pts])
+                left, right = traces(parts)
+                before = jnp.where(first, left, rolled(right, 1, 1))
+                after = jnp.where(last, right, rolled(left, -1, 1))
+                for p, value in zip(pts, slope(parts, before, after)):
+                    grad[v, p] = value
+            return carry
+
+        lax.fori_loop(0, 5, body, 0)
+        return carry
+
+    lax.fori_loop(0, count, normal_gradient, 0)
 
     row = lax.broadcasted_iota(jnp.int32, (rows, lanes), 0)
     for dx, dy in offsets:
@@ -396,12 +419,12 @@
                     pts = points(axis, q, j)
                     parts = fold([state[v, p] for p in pts])
                     left, right = traces(parts)
-                    jump_left = jnp.where(low, 0.0, rolled(right, step, 0)) - left
-                    jump_right = jnp.where(high, 0.0, rolled(left, -step, 0)) - right
+                    before = jnp.where(low, 0.0, rolled(right, step, 0))
+                    after = jnp.where(high, 0.0, rolled(left, -step, 0))
                     if axis == 0:
-                        jump_left = jnp.where(closed_low, 0.0, jump_left)
-                        jump_right = jnp.where(closed_high, 0.0, jump_right)
-                    gradient = slope(parts, jump_left, jump_right)
+                        before = jnp.where(closed_low, left, before)
+                        after = jnp.where(closed_high, right, after)
+                    gradient = slope(parts, before, after)
                     parts = fold([nu[p] * g for p, g in zip(pts, gradient)])
                     left, right = traces(parts)
                     store_pair(work, j, left, right, down, up, (v, 5 * q + j), *outer[axis])
@@ -410,7 +433,7 @@
                     if axis == 0:
                         before = jnp.where(closed_low, -left, before)
                         after = jnp.where(closed_high, -right, after)
-                    for p, value in zip(pts, slope(parts, before - left, after - right)):
+                    for p, value in zip(pts, slope(parts, before, after)):
                         if axis == 1:
                             acc[v, p] = value
                         else:
@@ -422,12 +445,6 @@
             return carry
 
         lax.fori_loop(0, count, variable, 0)
-
-    lane = lax.broadcasted_iota(jnp.int32, (rows, lanes), 1)
-    first, last = lane == 0, lane == lanes - 1
-
-    def store(v):
-        return pltpu.make_async_copy(acc.at[v], result.at[v], store_sem.at[v])
 
     for axis in range(2):
         low, high = masks[axis]
@@ -443,7 +460,7 @@
                 left, right = traces(parts)
                 edge[axis, 2 * f] = left
                 edge[axis, 2 * f + 1] = right
-                for i, value in enumerate(slope(parts, -left, -right)):
+                for i, value in enumerate(slope(parts, None, None)):
                     gain[axis, 5 * f + i] = value
             return carry
 
@@ -453,16 +470,11 @@
         def body(q, carry):
             for j in range(5):
                 pts = points(2, q, j)
-                parts = fold([state[v, p] for p in pts])
+                parts = fold([nu[p] * grad[v, p] for p in pts])
                 left, right = traces(parts)
-                jump_left = jnp.where(first, 0.0, rolled(right, 1, 1) - left)
-                jump_right = jnp.where(last, 0.0, rolled(left, -1, 1) - right)
-                gradient = slope(parts, jump_left, jump_right)
-                parts = fold([nu[p] * g for p, g in zip(pts, gradient)])
-                left, right = traces(parts)
-                jump_left = jnp.where(first, -left, rolled(right, 1, 1)) - left
-                jump_right = jnp.where(last, -right, rolled(left, -1, 1)) - right
-                for p, value in zip(pts, slope(parts, jump_left, jump_right)):
+                before = jnp.where(first, -left, rolled(right, 1, 1))
+                after = jnp.where(last, -right, rolled(left, -1, 1))
+                for p, value in zip(pts, slope(parts, before, after)):
                     acc[v, p] += value
             return carry
 
@@ -524,14 +536,10 @@
                 return carry
 
             lax.fori_loop(0, 5, body, 0)
-            if axis == 1:
-                store(v).start()
             return carry
 
         lax.fori_loop(0, count, correct, 0)
 
-    for v in range(count):
-        store(v).wait()
     for dx, dy in offsets:
         guarded(reachable(dx), lambda dx=dx, dy=dy: eps_copy(dx, dy).wait_send())
     for stage in range(2):
@@ -557,11 +565,10 @@
         return jax.ShapeDtypeStruct(shape, f32)
 
     vmem = pl.BlockSpec(memory_space=pltpu.VMEM)
-    hbm = pl.BlockSpec(memory_space=pl.ANY)
     nu, residual = pl.pallas_call(
         functools.partial(local_kernel, sizes, count, chords, spans),
         in_specs=[pl.BlockSpec(memory_space=pltpu.HBM)],
-        out_specs=[vmem, hbm],
+        out_specs=[vmem, vmem],
         out_shape=[full(npts, rows, lanes), full(count, npts, rows, lanes)],
         scratch_shapes=[
             pltpu.VMEM(shape, f32)
@@ -583,7 +590,6 @@
         ]
         + [
             pltpu.SemaphoreType.DMA((count,)),
-            pltpu.SemaphoreType.DMA((count,)),
             pltpu.SemaphoreType.DMA((9,)),
             pltpu.SemaphoreType.DMA((9,)),
             pltpu.SemaphoreType.DMA((2, 4, count)),

time: 30.1 us -> 22.4 us (0.74)
  Pallas kernels: 25.4 us -> 19.3 us
  local copies, waits for them, and re-layouts: 3.97 us -> 2.26 us
    pallas_call x1, Pallas kernels: 25.4 us -> 19.3 us  [shards(): pl.pallas_call(functools.partial(local_kernel, sizes, count, chords, span...]
    unnamed x4 -> x2, local copies, waits for them, and re-layouts: 3.97 us -> 2.26 us
where the time goes in v4:
time: 22.4 us; the launch traced here: 22.2 us
  Pallas kernels  19.3 us (86%)
  local copies, waits for them, and re-layouts  2.26 us (10%)
  between operations  0.64 us (3%)
    pallas_call x1, Pallas kernels, shards(): pl.pallas_call(functools.partial(local_kernel, sizes, count, chords, span...  19.3 us
    unnamed x2, local copies, waits for them, and re-layouts  2.26 us

profile of v4, /device:TPU:0, one launch (start us, length us, event | category | flops | bytes accessed | tf_op | source)
XLA Modules:
  0.0 22.2 jit_solution(10385829339606292071)
XLA Ops:
  0.6 19.3 %shard_map.30 = (f32[125,8,128]{2,1,0:T(8,128)S(1)}, f32[5,125,8,128]{3,2,1,0:T(8,128)S(1)}) custom-call(f32[5,125,8,128]{3,2,1,0:T(8,128)} %bitcast.5), custom_call_target="tpu_custom_call" | custom-call | tf_op jit(solution)/shard_map/pallas_call | solution.py:568
  20.0 1.5 %copy.5 = f32[5,125,4,2,128]{4,3,2,1,0:T(2,128)} copy(f32[5,125,4,2,128]{4,3,2,1,0:T(2,128)S(1)} %bitcast.3) | data formatting | bytes 5120000
  21.5 0.8 %copy.6 = f32[125,4,2,128]{3,2,1,0:T(2,128)} copy(f32[125,4,2,128]{3,2,1,0:T(2,128)S(1)} %bitcast.4) | data formatting | bytes 1024000

commit v5 on v4

--- a/solution.py
+++ b/solution.py
@@ -344,7 +344,7 @@
                     grad[v, p] = value
             return carry
 
-        lax.fori_loop(0, 5, body, 0)
+        lax.fori_loop(0, 5, body, 0, unroll=True)
         return carry
 
     lax.fori_loop(0, count, normal_gradient, 0)
@@ -440,7 +440,7 @@
                             acc[v, p] += value
                 return carry
 
-            lax.fori_loop(0, 5, body, 0)
+            lax.fori_loop(0, 5, body, 0, unroll=True)
             launch(1, axis, v)
             return carry
 
@@ -478,7 +478,7 @@
                     acc[v, p] += value
             return carry
 
-        lax.fori_loop(0, 5, body, 0)
+        lax.fori_loop(0, 5, body, 0, unroll=True)
         return carry
 
     lax.fori_loop(0, count, normal, 0)
@@ -535,7 +535,7 @@
                         acc[v, p] += gain[axis, 5 * f + i] * ghost + lifts[i]
                 return carry
 
-            lax.fori_loop(0, 5, body, 0)
+            lax.fori_loop(0, 5, body, 0, unroll=True)
             return carry
 
         lax.fori_loop(0, count, correct, 0)

time: 22.4 us -> 21.7 us (0.969)
  Pallas kernels: 19.3 us -> 18.7 us
    pallas_call x1, Pallas kernels: 19.3 us -> 18.7 us  [shards(): pl.pallas_call(functools.partial(local_kernel, sizes, count, chords, span...]
where the time goes in v5:
time: 21.7 us; the launch traced here: 21.6 us
  Pallas kernels  18.7 us (86%)
  local copies, waits for them, and re-layouts  2.26 us (10%)
  between operations  0.64 us (3%)
    pallas_call x1, Pallas kernels, shards(): pl.pallas_call(functools.partial(local_kernel, sizes, count, chords, span...  18.7 us
    unnamed x2, local copies, waits for them, and re-layouts  2.26 us

profile of v5, /device:TPU:0, one launch (start us, length us, event | category | flops | bytes accessed | tf_op | source)
XLA Modules:
  0.0 21.6 jit_solution(18401190923153131121)
XLA Ops:
  0.6 18.7 %shard_map.30 = (f32[125,8,128]{2,1,0:T(8,128)S(1)}, f32[5,125,8,128]{3,2,1,0:T(8,128)S(1)}) custom-call(f32[5,125,8,128]{3,2,1,0:T(8,128)} %bitcast.5), custom_call_target="tpu_custom_call" | custom-call | tf_op jit(solution)/shard_map/pallas_call | solution.py:568
  19.3 1.5 %copy.5 = f32[5,125,4,2,128]{4,3,2,1,0:T(2,128)} copy(f32[5,125,4,2,128]{4,3,2,1,0:T(2,128)S(1)} %bitcast.3) | data formatting | bytes 5120000
  20.8 0.8 %copy.6 = f32[125,4,2,128]{3,2,1,0:T(2,128)} copy(f32[125,4,2,128]{3,2,1,0:T(2,128)S(1)} %bitcast.4) | data formatting | bytes 1024000
